TPU v7x, 32 devices: a whole 2x2x4 slice. The times are simulated.
32 devices in a mesh: seq: 8 (over z, x), head: 4 (over y, core).
Axes of the slice: x: 2, y: 2, z: 4, core: 2. Of those that a mesh axis runs over, the one named last changes fastest.
Arguments:
- c_query: bfloat16 [256, 1536], P('seq', 'head'), may hold values from -60 to 60
- q_gain: float32 [1536], replicated, may hold values from 0.25 to 1.75
- w_query: bfloat16 [1536, 12288], P(None, 'head'), may hold values from -0.15625 to 0.15625
- kv_latent: bfloat16 [4096, 576], P('seq'), may hold values from -800 to 800
- kv_gain: float32 [512], replicated, may hold values from 0.25 to 1.75
- w_kv: bfloat16 [512, 16384], P(None, ('head', 'seq')), may hold values from -0.25 to 0.25
- w_out: bfloat16 [8192, 7168], P('head', 'seq'), may hold values from -0.5 to 0.5
- q_start: int32 [256], P('seq'), may hold values from 0 to 4095, as said below
Outputs:
- out: bfloat16 [256, 7168], P('head', 'seq')
Inputs may be any that keep to these rules, and one draw needn't show every extreme that they name: q_start[i] is at most pos_i and at least 512 * (i // 32 - 3); in every draw some query's q_start equals that lower limit. Within a block of 32 queries q_start never falls.
All inputs are finite; a program needn't handle non-finite values.
Results may differ from a plain program's by a relative error of at most 0.018.
The roundings to bfloat16 on the way count: a program that leaves them out, or rounds other values in their place, can miss the bound.
Values may be sent and summed in bfloat16 or wider, within the bound.
No kernel may reach another device: no remote copies, remote signals or barrier semaphores. Data moves between devices by JAX's collectives and lax.ppermute only.
A program may use at most 128 MiB of HBM per device.

v0:
```python
import functools

import jax
import jax.numpy as jnp
import numpy as np
from jax import lax
from jax.experimental import pallas as pl
from jax.experimental.pallas import tpu as pltpu
from jax.sharding import PartitionSpec as P


KVL = 512
NOPE = 128
ROPE = 64
VDIM = 128
REACH = 3
DIGIT = 64
STAGE_LIMIT = 52000 << 10


EPS = 1e-06
THETA = 10000.0


def passed_along(x, axis, by):
    devices = lax.axis_size(axis)
    pairs = [(i, i + by) for i in range(devices) if 0 <= i + by < devices]
    return lax.ppermute(x, axis, pairs)


def rms_scale(latent_rows, gain_row):
    values = latent_rows.astype(jnp.float32)
    mean_square = jnp.mean(values * values, axis=-1, keepdims=True)
    return values * lax.rsqrt(mean_square + EPS) * gain_row


def rotate(rotary, position):
    half_size = rotary.shape[-1] // 2
    exponent = jnp.arange(half_size, dtype=jnp.float32) * (2.0 / rotary.shape[-1])
    angles = position.astype(jnp.float32)[:, None] * (THETA ** (-exponent))[None, :]
    cosine = jnp.cos(angles)[:, None, :]
    sine_of = jnp.sin(angles)[:, None, :]
    former = rotary[..., :half_size]
    latter = rotary[..., half_size:]
    return jnp.concatenate(
        [former * cosine - latter * sine_of, latter * cosine + former * sine_of], axis=-1
    )


def masked_scores(query_block, starts, places, key_heads, rope_keys, first_key):
    key_place = first_key + jnp.arange(key_heads.shape[0], dtype=jnp.int32)
    scores = jnp.einsum(
        "qhd,khd->hqk",
        query_block[..., :NOPE],
        key_heads[..., :NOPE],
        preferred_element_type=jnp.float32,
    )
    scores = scores + jnp.einsum(
        "qhd,kd->hqk", query_block[..., NOPE:], rope_keys, preferred_element_type=jnp.float32
    )
    scores = scores * (NOPE + ROPE) ** (-0.5)
    allowed = (key_place[None, :] >= starts[:, None]) & (key_place[None, :] <= places[:, None])
    return (jnp.where(allowed[None], scores, -jnp.inf), allowed)


def body(c_query, q_gain, w_query, kv_latent, kv_gain, w_kv, w_out, q_start):
    query_rows = c_query.shape[0]
    key_rows = kv_latent.shape[0]
    head_count = w_query.shape[1] // (NOPE + ROPE)
    block_index = lax.axis_index("seq")
    full_query = lax.all_gather(c_query, "head", axis=1, tiled=True)
    normed = rms_scale(full_query, q_gain).astype(jnp.bfloat16)
    query_raw = jnp.dot(normed, w_query, preferred_element_type=jnp.float32).reshape(
        query_rows, head_count, NOPE + ROPE
    )
    position = (
        block_index * key_rows + key_rows - query_rows + jnp.arange(query_rows, dtype=jnp.int32)
    )
    query_all = jnp.concatenate(
        [query_raw[..., :NOPE], rotate(query_raw[..., NOPE:], position)], axis=-1
    ).astype(jnp.bfloat16)
    kv_weights = lax.all_gather(w_kv, "seq", axis=1, tiled=True)

    def project(latent_block):
        scaled = rms_scale(latent_block, kv_gain).astype(jnp.bfloat16)
        return jnp.dot(scaled, kv_weights, preferred_element_type=jnp.float32).astype(jnp.bfloat16)

    own_heads = project(kv_latent[:, :KVL])
    own_rope = kv_latent[:, KVL:]
    head_parts = [own_heads]
    rope_parts = [own_rope]
    for offset in range(1, REACH + 1):
        moved_block = passed_along(kv_latent, "seq", offset)
        head_parts.insert(0, project(moved_block[:, :KVL]))
        rope_parts.insert(0, moved_block[:, KVL:])
    window_blocks = REACH + 1
    key_heads = jnp.concatenate(head_parts, axis=0).reshape(
        window_blocks * key_rows, head_count, NOPE + VDIM
    )
    rope_keys = jnp.concatenate(rope_parts, axis=0)
    scores, _ = masked_scores(
        query_all, q_start, position, key_heads, rope_keys, (block_index - REACH) * key_rows
    )
    largest = jnp.max(scores, axis=-1, keepdims=True)
    exponent_terms = jnp.exp(scores - largest)
    weights_bf = (exponent_terms / jnp.sum(exponent_terms, axis=-1, keepdims=True)).astype(
        jnp.bfloat16
    )
    attended = jnp.einsum(
        "hqk,khd->qhd", weights_bf, key_heads[..., NOPE:], preferred_element_type=jnp.float32
    )
    attended = attended.astype(jnp.bfloat16).reshape(query_rows, head_count * VDIM)
    partial_rows = jnp.dot(
        lax.all_gather(attended, "seq", axis=0, tiled=True),
        w_out,
        preferred_element_type=jnp.float32,
    )
    return lax.psum_scatter(partial_rows, "head", scatter_dimension=0, tiled=True).astype(
        jnp.bfloat16
    )


def exchanged(x, seq_flip, head_flip=0):
    if not head_flip:
        axes, flip, devices = "seq", seq_flip, lax.axis_size("seq")
    elif not seq_flip:
        axes, flip, devices = "head", head_flip, lax.axis_size("head")
    else:
        head = lax.axis_size("head")
        axes, flip = ("seq", "head"), seq_flip * head + head_flip
        devices = lax.axis_size("seq") * head
    return lax.ppermute(x, axes, [(i, i ^ flip) for i in range(devices)])


def pack_kernel(
    start_hbm, gain_hbm, query_hbm, latent_hbm, packed_ref, start_ref, gain_ref, query_ref, columns, sems
):
    rows = columns.shape[1]
    head_at = lax.axis_index("head")
    copy = pltpu.make_async_copy(
        latent_hbm.at[:, pl.ds(pl.multiple_of(head_at * rows, rows), rows)], columns, sems.at[0]
    )
    gain_copy = pltpu.make_async_copy(gain_hbm, gain_ref, sems.at[1])
    query_copy = pltpu.make_async_copy(query_hbm, query_ref, sems.at[2])
    start_copy = pltpu.make_async_copy(start_hbm, start_ref, sems.at[3])
    copies = (copy, gain_copy, query_copy, start_copy)
    for each in copies:
        each.start()
    for each in copies[1:]:
        each.wait()
    half = KVL // 2
    quarter = rows // 4
    query_rows = query_ref.shape[0]
    query_at = 2 * rows + quarter
    packed_ref[query_at : query_at + query_rows, :] = query_ref[:, :half]
    fold_at = query_at + query_rows
    folded = query_rows // 2
    packed_ref[fold_at : fold_at + folded, :] = jnp.concatenate(
        [query_ref[:folded, half:], query_ref[folded:, half:]], axis=1
    )
    start_at = fold_at + folded
    share = packed_ref.shape[0] - start_at
    window_first = (lax.axis_index("seq") - REACH) * (rows * (query_rows // share))
    shape = (share, half)
    row = lax.broadcasted_iota(jnp.int32, shape, 0)
    offset = jnp.zeros(shape, jnp.int32)
    for r in range(share):
        offset = jnp.where(row == r, start_ref[head_at * share + r] - window_first, offset)
    high = offset // DIGIT
    digit = jnp.where(
        lax.broadcasted_iota(jnp.int32, shape, 1) < half // 2, high, offset - high * DIGIT
    )
    packed_ref[start_at:, :] = digit.astype(jnp.float32).astype(jnp.bfloat16)
    copy.wait()
    values = columns[:KVL, :].astype(jnp.float32).T
    mean_square = jnp.mean(values * values, axis=-1, keepdims=True)
    normed = (values * lax.rsqrt(mean_square + EPS) * gain_ref[...]).astype(jnp.bfloat16)
    packed_ref[:rows, :] = normed[:, :half]
    packed_ref[rows : 2 * rows, :] = normed[:, half:]
    rope = columns[KVL:, :].astype(jnp.float32).T.astype(jnp.bfloat16)
    packed_ref[2 * rows : query_at, :] = jnp.concatenate(
        [rope[g * quarter : (g + 1) * quarter] for g in range(4)], axis=1
    )


def pack(kv_latent, kv_gain, c_query, q_start):
    head_devices = lax.axis_size("head")
    rows = kv_latent.shape[0] // head_devices
    query_rows = c_query.shape[0]
    packed_rows = 2 * rows + rows // 4 + query_rows + query_rows // 2 + query_rows // head_devices
    return pl.pallas_call(
        pack_kernel,
        out_shape=jax.ShapeDtypeStruct((packed_rows, KVL // 2), jnp.bfloat16),
        in_specs=[pl.BlockSpec(memory_space=pltpu.HBM)] * 4,
        out_specs=pl.BlockSpec(memory_space=pltpu.VMEM),
        scratch_shapes=[
            pltpu.SMEM(q_start.shape, jnp.int32),
            pltpu.VMEM((1, KVL), jnp.float32),
            pltpu.VMEM(c_query.shape, jnp.bfloat16),
            pltpu.VMEM((kv_latent.shape[1], rows), jnp.bfloat16),
            pltpu.SemaphoreType.DMA((4,)),
        ],
        name="pack",
    )(q_start, kv_gain.reshape(1, KVL), c_query, kv_latent.T)


HOPS = (
    ((0, 0), (4, 0)),
    ((0, 0), (2, 0)),
    ((0, 0), (1, 0)),
    ((0, 0), (0, 2)),
    ((1, 0), (0, 2)),
    ((2, 0), (1, 0)),
    ((2, 0), (0, 2)),
    ((4, 0), (2, 0)),
    ((4, 0), (1, 0)),
    ((4, 0), (0, 2)),
    ((2, 2), (1, 0)),
    ((6, 0), (1, 0)),
    ((6, 0), (0, 2)),
    ((5, 0), (0, 2)),
    ((6, 2), (1, 0)),
)


def gather_pieces(own):
    got = {(0, 0): own}
    for source, flip in HOPS:
        got[source[0] ^ flip[0], source[1] ^ flip[1]] = exchanged(got[source], *flip)
    for (seq_flip, head_flip), v in list(got.items()):
        got[seq_flip, head_flip + 1] = exchanged(v, 0, 1)
    return got


def stage_kernel(w_query_hbm, w_kv_hbm, gain_hbm, turn_hbm, w_query, w_kv, gain, turn, sems):
    columns = w_query.shape[1]
    left = pl.multiple_of(lax.axis_index("seq") * columns, 128)
    copies = (
        pltpu.make_async_copy(w_query_hbm.at[:, pl.ds(left, columns)], w_query, sems.at[0]),
        pltpu.make_async_copy(w_kv_hbm, w_kv, sems.at[1]),
        pltpu.make_async_copy(gain_hbm, gain, sems.at[2]),
        pltpu.make_async_copy(turn_hbm, turn, sems.at[3]),
    )
    for each in copies:
        each.start()
    for each in copies:
        each.wait()


def stage(w_query, w_kv, q_gain, turn):
    columns = w_kv.shape[1] // (NOPE + VDIM) * (NOPE + ROPE)
    vmem = pl.BlockSpec(memory_space=pltpu.VMEM)
    return pl.pallas_call(
        stage_kernel,
        out_shape=[
            jax.ShapeDtypeStruct((w_query.shape[0], columns), jnp.bfloat16),
            jax.ShapeDtypeStruct(w_kv.shape, jnp.bfloat16),
            jax.ShapeDtypeStruct(q_gain.shape, jnp.float32),
            jax.ShapeDtypeStruct(turn.shape, jnp.float32),
        ],
        in_specs=[pl.BlockSpec(memory_space=pltpu.HBM)] * 4,
        out_specs=[vmem] * 4,
        scratch_shapes=[pltpu.SemaphoreType.DMA((4,))],
        compiler_params=pltpu.CompilerParams(vmem_limit_bytes=STAGE_LIMIT),
        name="stage",
    )(w_query, w_kv, q_gain, turn)


def attend_kernel(flips, blocks, *refs):
    pieces = dict(zip(flips, refs[: len(flips)]))
    (w_query, w_kv_ref, gain_ref, turn_ref, out_ref) = refs[len(flips) : len(flips) + 5]
    (latent_query, starts, queries, keys, values, scores, probs) = refs[len(flips) + 5 :]
    seq_at = lax.axis_index("seq")
    head_at = lax.axis_index("head")
    parts = len(flips) // blocks
    heads = queries.shape[0]
    wide = NOPE + ROPE
    query_rows = queries.shape[1] // blocks
    key_rows = keys.shape[1] // blocks
    rows = key_rows // parts
    half = KVL // 2
    quarter = rows // 4
    rope_at = 2 * rows
    query_at = rope_at + quarter
    fold_at = query_at + query_rows
    folded = query_rows // 2
    start_at = fold_at + folded
    share = query_rows // parts
    query_wide = latent_query.shape[1] // parts
    rest = query_wide - half
    for seq_flip in range(blocks):
        top = pl.multiple_of((seq_at ^ seq_flip) * query_rows, query_rows)
        for f in range(parts):
            piece = pieces[seq_flip, f]
            part = head_at ^ f
            at = pl.multiple_of(part * query_wide, 128)
            latent_query[pl.ds(top, query_rows), pl.ds(at, half)] = piece[query_at:fold_at, :]
            at = pl.multiple_of(at + half, 128)
            for g in range(2):
                latent_query[pl.ds(top + g * folded, folded), pl.ds(at, rest)] = piece[
                    fold_at:start_at, g * rest : (g + 1) * rest
                ]
            to = pl.multiple_of(top + part * share, share)
            starts[pl.ds(to, share), :] = piece[start_at:, :].astype(jnp.float32)

    for seq_flip in range(blocks):
        key_top = pl.multiple_of((seq_at ^ seq_flip) * key_rows, key_rows)
        low = jnp.concatenate([pieces[seq_flip, f][:rows, :] for f in range(parts)], axis=0)
        high = jnp.concatenate(
            [pieces[seq_flip, f][rows : 2 * rows, :] for f in range(parts)], axis=0
        )
        both = jnp.dot(low, w_kv_ref[:half, :], preferred_element_type=jnp.float32) + jnp.dot(
            high, w_kv_ref[half:, :], preferred_element_type=jnp.float32
        )
        both = both.astype(jnp.bfloat16)
        for f in range(parts):
            piece = pieces[seq_flip, f]
            to = pl.multiple_of(key_top + (head_at ^ f) * rows, rows)
            span = slice(f * rows, (f + 1) * rows)
            rope = jnp.concatenate(
                [piece[rope_at:query_at, g * ROPE : (g + 1) * ROPE] for g in range(4)], axis=0
            )
            for j in range(heads):
                left = j * (NOPE + VDIM)
                keys[j, pl.ds(to, rows), :NOPE] = both[span, left : left + NOPE]
                keys[j, pl.ds(to, rows), NOPE:] = rope
                values[j, pl.ds(to, rows), :] = both[span, left + NOPE : left + NOPE + VDIM]

    for b in range(blocks):
        span = slice(b * query_rows, (b + 1) * query_rows)
        wide_rows = latent_query[span, :].astype(jnp.float32)
        mean_square = jnp.mean(wide_rows * wide_rows, axis=-1, keepdims=True)
        latent_query[span, :] = (
            wide_rows * lax.rsqrt(mean_square + EPS) * gain_ref[...].reshape(1, -1)
        ).astype(jnp.bfloat16)
    raw = jnp.dot(latent_query[...], w_query[...], preferred_element_type=jnp.float32)
    for j in range(heads):
        head_raw = raw[:, j * wide : (j + 1) * wide]
        queries[j, :, :NOPE] = head_raw[:, :NOPE].astype(jnp.bfloat16)
        rotary = head_raw[:, NOPE:]
        crossed = jnp.concatenate([rotary[:, ROPE // 2 :], rotary[:, : ROPE // 2]], axis=1)
        queries[j, :, NOPE:] = (
            rotary * turn_ref[:, :ROPE] + crossed * turn_ref[:, ROPE:]
        ).astype(jnp.bfloat16)

    def score(b):
        count = min(REACH + 1, blocks - b) * query_rows
        for j in range(heads):
            scores[j, b, :count, :] = lax.dot_general(
                queries[j, b * query_rows : b * query_rows + count, :],
                keys[j, b * key_rows : (b + 1) * key_rows, :],
                (((1,), (1,)), ((), ())),
                preferred_element_type=jnp.float32,
            )

    def soften(b):
        digits = starts[b * query_rows : (b + 1) * query_rows, :]
        offset = digits[:, :128] * DIGIT + digits[:, half // 2 : half // 2 + 128]
        start = jnp.concatenate([offset] * (key_rows // 128), axis=1).astype(jnp.int32)
        window = range(max(b - REACH, 0), b + 1)
        shape = (query_rows, key_rows)
        column = lax.broadcasted_iota(jnp.int32, shape, 1)
        row = lax.broadcasted_iota(jnp.int32, shape, 0)
        for j in range(heads):
            masked = []
            for w in window:
                top = (b - w) * query_rows
                part = scores[j, w, top : top + query_rows, :] * wide ** (-0.5)
                allowed = column >= start - (w - b + REACH) * key_rows
                if w == b:
                    allowed = allowed & (column <= row + (key_rows - query_rows))
                masked.append(jnp.where(allowed, part, -jnp.inf))
            largest = masked[0]
            for part in masked[1:]:
                largest = jnp.maximum(largest, part)
            largest = jnp.max(largest, axis=-1, keepdims=True)
            terms = [jnp.exp(part - largest) for part in masked]
            total = terms[0]
            for part in terms[1:]:
                total = total + part
            inverse = 1.0 / jnp.sum(total, axis=-1, keepdims=True)
            for w, part in zip(window, terms):
                top = (b - w) * query_rows
                probs[j, w, top : top + query_rows, :] = (part * inverse).astype(jnp.bfloat16)

    for b in range(blocks):
        score(b)
        soften(b)
    for j in range(heads):
        sums = [None] * blocks
        for w in range(blocks):
            count = min(REACH + 1, blocks - w)
            mixed = jnp.dot(
                probs[j, w, : count * query_rows, :],
                values[j, w * key_rows : (w + 1) * key_rows, :],
                preferred_element_type=jnp.float32,
            )
            for i in range(count):
                part = mixed[i * query_rows : (i + 1) * query_rows]
                sums[w + i] = part if sums[w + i] is None else sums[w + i] + part
            out_ref[w * query_rows : (w + 1) * query_rows, j * VDIM : (j + 1) * VDIM] = sums[
                w
            ].astype(jnp.bfloat16)


def attend(got, weights, query_rows, key_rows):
    blocks = lax.axis_size("seq")
    w_query, w_kv, _, _ = weights
    flips = tuple(sorted(got))
    pieces = [got[f] for f in flips]
    heads = w_kv.shape[1] // (NOPE + VDIM)
    wide = NOPE + ROPE
    queries = blocks * query_rows
    keys = key_rows * blocks
    count = (REACH + 1) * query_rows
    vmem = pl.BlockSpec(memory_space=pltpu.VMEM)
    return pl.pallas_call(
        functools.partial(attend_kernel, flips, blocks),
        out_shape=jax.ShapeDtypeStruct((queries, heads * VDIM), jnp.bfloat16),
        in_specs=[vmem] * (len(flips) + len(weights)),
        out_specs=vmem,
        scratch_shapes=[
            pltpu.VMEM((queries, w_query.shape[0]), jnp.bfloat16),
            pltpu.VMEM((queries, KVL // 2), jnp.float32),
            pltpu.VMEM((heads, queries, wide), jnp.bfloat16),
            pltpu.VMEM((heads, keys, wide), jnp.bfloat16),
            pltpu.VMEM((heads, keys, VDIM), jnp.bfloat16),
            pltpu.VMEM((heads, blocks, count, key_rows), jnp.float32),
            pltpu.VMEM((heads, blocks, count, key_rows), jnp.bfloat16),
        ],
        compiler_params=pltpu.CompilerParams(vmem_limit_bytes=32 << 20),
        name="attend",
    )(*pieces, *weights)


def project_out_kernel(blocks, *refs):
    pieces = refs[:blocks]
    w_out_ref = refs[blocks]
    outs = refs[blocks + 1 : -1]
    summed = refs[-1]
    seq_at = lax.axis_index("seq")
    head_at = lax.axis_index("head")
    features = pieces[0].shape[1]
    columns = w_out_ref.shape[1]
    for left in range(0, columns, 256):
        span = slice(left, min(left + 256, columns))
        total = None
        for flip in range(blocks):
            top = pl.multiple_of((seq_at ^ flip) * features, features)
            part = jnp.dot(
                pieces[flip][...],
                w_out_ref[pl.ds(top, features), span],
                preferred_element_type=jnp.float32,
            )
            total = part if total is None else total + part
        summed[:, span] = total
    rows = outs[0].shape[0]
    for flip, out_ref in enumerate(outs):
        top = pl.multiple_of((head_at ^ flip) * rows, rows)
        out_ref[...] = summed[pl.ds(top, rows), :].astype(out_ref.dtype)


def project_out(pieces, w_out):
    owners = lax.axis_size("head")
    queries = pieces[0].shape[0]
    columns = w_out.shape[1]
    vmem = pl.BlockSpec(memory_space=pltpu.VMEM)
    return pl.pallas_call(
        functools.partial(project_out_kernel, len(pieces)),
        out_shape=[
            jax.ShapeDtypeStruct((queries // owners, columns), jnp.bfloat16 if k else jnp.float32)
            for k in range(owners)
        ],
        in_specs=[vmem] * (len(pieces) + 1),
        out_specs=[vmem] * owners,
        scratch_shapes=[pltpu.VMEM((queries, columns), jnp.float32)],
        compiler_params=pltpu.CompilerParams(vmem_limit_bytes=16 << 20),
        name="project_out",
    )(*pieces, w_out)


SPREAD_HOPS = ((0, 4), (0, 1), (0, 2), (1, 2), (4, 2), (4, 1), (4, 3))


def rotation_table(blocks, query_rows, key_rows):
    serial = np.arange(blocks * query_rows)
    position = serial // query_rows * key_rows + key_rows - query_rows + serial % query_rows
    angles = position[:, None] * THETA ** (-np.arange(ROPE // 2) * (2.0 / ROPE))[None, :]
    cosine, sine_of = np.cos(angles), np.sin(angles)
    return np.concatenate([cosine, cosine, -sine_of, sine_of], axis=1).astype(np.float32)


def heads_body(c_query, q_gain, w_query, kv_latent, kv_gain, w_kv, w_out, q_start):
    blocks = lax.axis_size("seq")
    query_rows = c_query.shape[0]
    key_rows = kv_latent.shape[0]
    own = pack(kv_latent, kv_gain, c_query, q_start)
    weights = stage(w_query, w_kv, q_gain, rotation_table(blocks, query_rows, key_rows))
    got = gather_pieces(own)
    attended = attend(got, weights, query_rows, key_rows)
    spread = {0: attended}
    for source, flip in SPREAD_HOPS:
        spread[source ^ flip] = exchanged(spread[source], flip)
    shares = project_out([spread[k] for k in range(blocks)], w_out)
    total = shares[0]
    for k in range(1, len(shares)):
        total = total + exchanged(shares[k], 0, k).astype(jnp.float32)
    return total.astype(jnp.bfloat16)


def solution(mesh):
    in_specs = (
        P("seq", "head"),
        P(),
        P(None, "head"),
        P("seq", None),
        P(),
        P(None, ("head", "seq")),
        P("head", "seq"),
        P("seq"),
    )
    out_specs = P("head", "seq")

    def layer(*args):
        _, _, _, _, _, w_kv, _, _ = args
        seq, heads = mesh.shape["seq"], mesh.shape["head"]
        own_columns = w_kv.shape[1] // (seq * heads)
        whole_heads = own_columns % (NOPE + VDIM) == 0
        by_heads = whole_heads and (seq, heads) == (8, 4)
        step = jax.shard_map(
            heads_body if by_heads else body,
            mesh=mesh,
            in_specs=in_specs,
            out_specs=out_specs,
            check_vma=False,
        )
        return step(*args)

    return layer
```

profile of v0, /device:TPU:0, one launch (start us, length us, event | category | flops | bytes accessed | tf_op | source)
XLA Modules:
  0.0 86.0 jit_solution(15434754967715806411)
XLA Ops:
  0.0 1.9 %pack.1.refs_0_ = bf16[344,256]{1,0:T(8,128)(2,1)} custom-call(s32[32]{0:T(128)} %start_hbm.1, f32[1,512]{1,0:T(1,128)} %bitcast.3, bf16[32,384]{1,0:T(8,128)(2,1)} %query_hbm.1, bf16[576,512]{1,0:T(8,128)(2,1)} %bitcast.2), custom_call_target="tpu_custom_call" | custom-call | tf_op jit(solution)/shard_map/pack/pallas_call | solution.py:191
  1.9 4.1 %collective-permute-start.15 = (bf16[344,256]{1,0:T(8,128)(2,1)}, bf16[344,256]{1,0:T(8,128)(2,1)S(1)}, u32[]{:S(2)}, u32[]{:S(2)}) collective-permute-start(bf16[344,256]{1,0:T(8,128)(2,1)} %pack.1.refs_0_), channel_id=1, source_target_pairs={{0,16},{4,20},{8,24},{12,28},{16,0},{20,4},{24,8},{28,12},{1,17},{... | collective-permute-start | bytes 528392 | tf_op jit(solution)/shard_map/ppermute | solution.py:132
  6.0 1.6 %collective-permute-start.7 = (bf16[344,256]{1,0:T(8,128)(2,1)}, bf16[344,256]{1,0:T(8,128)(2,1)S(1)}, u32[]{:S(2)}, u32[]{:S(2)}) collective-permute-start(bf16[344,256]{1,0:T(8,128)(2,1)} %pack.1.refs_0_), channel_id=1, source_target_pairs={{0,8},{4,12},{8,0},{12,4},{16,24},{20,28},{24,16},{28,20},{1,9},{5... | collective-permute-start | bytes 528392 | tf_op jit(solution)/shard_map/ppermute | solution.py:132
  7.6 1.5 %collective-permute-start.3 = (bf16[344,256]{1,0:T(8,128)(2,1)}, bf16[344,256]{1,0:T(8,128)(2,1)S(1)}, u32[]{:S(2)}, u32[]{:S(2)}) collective-permute-start(bf16[344,256]{1,0:T(8,128)(2,1)} %pack.1.refs_0_), channel_id=1, source_target_pairs={{0,4},{4,0},{8,12},{12,8},{16,20},{20,16},{24,28},{28,24},{1,5},{5... | collective-permute-start | bytes 528392 | tf_op jit(solution)/shard_map/ppermute | solution.py:132
  9.1 1.5 %collective-permute-start.1 = (bf16[344,256]{1,0:T(8,128)(2,1)}, bf16[344,256]{1,0:T(8,128)(2,1)S(1)}, u32[]{:S(2)}, u32[]{:S(2)}) collective-permute-start(bf16[344,256]{1,0:T(8,128)(2,1)} %pack.1.refs_0_), channel_id=1, source_target_pairs={{0,2},{1,3},{2,0},{3,1},{4,6},{5,7},{6,4},{7,5},{8,10},{9,11},{10,... | collective-permute-start | bytes 528392 | tf_op jit(solution)/shard_map/ppermute | solution.py:132
  10.6 4.0 %collective-permute-done.15.refs_16_ = bf16[344,256]{1,0:T(8,128)(2,1)S(1)} collective-permute-done((bf16[344,256]{1,0:T(8,128)(2,1)}, bf16[344,256]{1,0:T(8,128)(2,1)S(1)}, u32[]{:S(2)}, u32[]{:S(2)}) %collective-permute-start.15) | collective-permute-done | bytes 176160 | tf_op jit(solution)/shard_map/ppermute | solution.py:132
  14.6 0.7 collective-permute-start.23
  15.3 1.5 %collective-permute-start.19 = (bf16[344,256]{1,0:T(8,128)(2,1)S(1)}, bf16[344,256]{1,0:T(8,128)(2,1)S(1)}, u32[]{:S(2)}, u32[]{:S(2)}) collective-permute-start(bf16[344,256]{1,0:T(8,128)(2,1)S(1)} %collective-permute-done.15.refs_16_), channel_id=1, source_target_pairs={{0,4},{4,0},{8,12},{12,8},{16,20},{20,16},{24,28},{28,24},{1,5},{5... | collective-permute-start | bytes 528392 | tf_op jit(solution)/shard_map/ppermute | solution.py:132
  16.8 1.5 %collective-permute-start.17 = (bf16[344,256]{1,0:T(8,128)(2,1)S(1)}, bf16[344,256]{1,0:T(8,128)(2,1)S(1)}, u32[]{:S(2)}, u32[]{:S(2)}) collective-permute-start(bf16[344,256]{1,0:T(8,128)(2,1)S(1)} %collective-permute-done.15.refs_16_), channel_id=1, source_target_pairs={{0,2},{1,3},{2,0},{3,1},{4,6},{5,7},{6,4},{7,5},{8,10},{9,11},{10,... | collective-permute-start | bytes 528392 | tf_op jit(solution)/shard_map/ppermute | solution.py:132
  18.3 0.6 collective-permute-start.11
  18.9 1.2 %collective-permute-done.23.refs_24_ = bf16[344,256]{1,0:T(8,128)(2,1)S(1)} collective-permute-done((bf16[344,256]{1,0:T(8,128)(2,1)S(1)}, bf16[344,256]{1,0:T(8,128)(2,1)S(1)}, u32[]{:S(2)}, u32[]{:S(2)}) %collective-permute-start.23) | collective-permute-done | bytes 176160 | tf_op jit(solution)/shard_map/ppermute | solution.py:132
  20.1 1.5 %collective-permute-start.9 = (bf16[344,256]{1,0:T(8,128)(2,1)S(1)}, bf16[344,256]{1,0:T(8,128)(2,1)S(1)}, u32[]{:S(2)}, u32[]{:S(2)}) collective-permute-start(bf16[344,256]{1,0:T(8,128)(2,1)S(1)} %collective-permute-done.7.refs_8_), channel_id=1, source_target_pairs={{0,2},{1,3},{2,0},{3,1},{4,6},{5,7},{6,4},{7,5},{8,10},{9,11},{10,... | collective-permute-start | bytes 528392 | tf_op jit(solution)/shard_map/ppermute | solution.py:132
  21.6 2.0 %collective-permute-done.17.refs_18_ = bf16[344,256]{1,0:T(8,128)(2,1)S(1)} collective-permute-done((bf16[344,256]{1,0:T(8,128)(2,1)S(1)}, bf16[344,256]{1,0:T(8,128)(2,1)S(1)}, u32[]{:S(2)}, u32[]{:S(2)}) %collective-permute-start.17) | collective-permute-done | bytes 176160 | tf_op jit(solution)/shard_map/ppermute | solution.py:132
  23.6 2.1 %collective-permute-start.5 = (bf16[344,256]{1,0:T(8,128)(2,1)S(1)}, bf16[344,256]{1,0:T(8,128)(2,1)S(1)}, u32[]{:S(2)}, u32[]{:S(2)}) collective-permute-start(bf16[344,256]{1,0:T(8,128)(2,1)S(1)} %collective-permute-done.3.refs_4_), channel_id=1, source_target_pairs={{0,2},{1,3},{2,0},{3,1},{4,6},{5,7},{6,4},{7,5},{8,10},{9,11},{10,... | collective-permute-start | bytes 528392 | tf_op jit(solution)/shard_map/ppermute | solution.py:132
  25.7 0.5 collective-permute-start.2
  26.2 1.3 %collective-permute-done.9.refs_10_ = bf16[344,256]{1,0:T(8,128)(2,1)S(1)} collective-permute-done((bf16[344,256]{1,0:T(8,128)(2,1)S(1)}, bf16[344,256]{1,0:T(8,128)(2,1)S(1)}, u32[]{:S(2)}, u32[]{:S(2)}) %collective-permute-start.9) | collective-permute-done | bytes 176160 | tf_op jit(solution)/shard_map/ppermute | solution.py:132
  27.5 1.4 %collective-permute-start.25 = (bf16[344,256]{1,0:T(8,128)(2,1)S(1)}, bf16[344,256]{1,0:T(8,128)(2,1)S(1)}, u32[]{:S(2)}, u32[]{:S(2)}) collective-permute-start(bf16[344,256]{1,0:T(8,128)(2,1)S(1)} %collective-permute-done.23.refs_24_), channel_id=1, source_target_pairs={{0,2},{1,3},{2,0},{3,1},{4,6},{5,7},{6,4},{7,5},{8,10},{9,11},{10,... | collective-permute-start | bytes 528392 | tf_op jit(solution)/shard_map/ppermute | solution.py:132
  28.8 2.0 %collective-permute-done.5.refs_6_ = bf16[344,256]{1,0:T(8,128)(2,1)S(1)} collective-permute-done((bf16[344,256]{1,0:T(8,128)(2,1)S(1)}, bf16[344,256]{1,0:T(8,128)(2,1)S(1)}, u32[]{:S(2)}, u32[]{:S(2)}) %collective-permute-start.5) | collective-permute-done | bytes 176160 | tf_op jit(solution)/shard_map/ppermute | solution.py:132
  30.9 1.5 %collective-permute-start.21 = (bf16[344,256]{1,0:T(8,128)(2,1)S(1)}, bf16[344,256]{1,0:T(8,128)(2,1)S(1)}, u32[]{:S(2)}, u32[]{:S(2)}) collective-permute-start(bf16[344,256]{1,0:T(8,128)(2,1)S(1)} %collective-permute-done.19.refs_20_), channel_id=1, source_target_pairs={{0,2},{1,3},{2,0},{3,1},{4,6},{5,7},{6,4},{7,5},{8,10},{9,11},{10,... | collective-permute-start | bytes 528392 | tf_op jit(solution)/shard_map/ppermute | solution.py:132
  32.9 1.1 %collective-permute-done.25.refs_26_ = bf16[344,256]{1,0:T(8,128)(2,1)S(1)} collective-permute-done((bf16[344,256]{1,0:T(8,128)(2,1)S(1)}, bf16[344,256]{1,0:T(8,128)(2,1)S(1)}, u32[]{:S(2)}, u32[]{:S(2)}) %collective-permute-start.25) | collective-permute-done | bytes 176160 | tf_op jit(solution)/shard_map/ppermute | solution.py:132
  34.0 1.5 %collective-permute-start.13 = (bf16[344,256]{1,0:T(8,128)(2,1)S(1)}, bf16[344,256]{1,0:T(8,128)(2,1)S(1)}, u32[]{:S(2)}, u32[]{:S(2)}) collective-permute-start(bf16[344,256]{1,0:T(8,128)(2,1)S(1)} %collective-permute-done.9.refs_10_), channel_id=1, source_target_pairs={{0,4},{4,0},{8,12},{12,8},{16,20},{20,16},{24,28},{28,24},{1,5},{5... | collective-permute-start | bytes 528392 | tf_op jit(solution)/shard_map/ppermute | solution.py:132
  35.5 2.2 %collective-permute-done.21.refs_22_ = bf16[344,256]{1,0:T(8,128)(2,1)S(1)} collective-permute-done((bf16[344,256]{1,0:T(8,128)(2,1)S(1)}, bf16[344,256]{1,0:T(8,128)(2,1)S(1)}, u32[]{:S(2)}, u32[]{:S(2)}) %collective-permute-start.21) | collective-permute-done | bytes 176160 | tf_op jit(solution)/shard_map/ppermute | solution.py:132
  37.7 0.5 collective-permute-start.6
  38.2 1.0 %collective-permute-start.29 = (bf16[344,256]{1,0:T(8,128)(2,1)S(1)}, bf16[344,256]{1,0:T(8,128)(2,1)S(1)}, u32[]{:S(2)}, u32[]{:S(2)}) collective-permute-start(bf16[344,256]{1,0:T(8,128)(2,1)S(1)} %collective-permute-done.25.refs_26_), channel_id=1, source_target_pairs={{0,4},{4,0},{8,12},{12,8},{16,20},{20,16},{24,28},{28,24},{1,5},{5... | collective-permute-start | bytes 528392 | tf_op jit(solution)/shard_map/ppermute | solution.py:132
  39.2 1.6 %collective-permute-done.13.refs_14_ = bf16[344,256]{1,0:T(8,128)(2,1)S(1)} collective-permute-done((bf16[344,256]{1,0:T(8,128)(2,1)S(1)}, bf16[344,256]{1,0:T(8,128)(2,1)S(1)}, u32[]{:S(2)}, u32[]{:S(2)}) %collective-permute-start.13) | collective-permute-done | bytes 176160 | tf_op jit(solution)/shard_map/ppermute | solution.py:132
  40.8 0.5 collective-permute-start.22
  41.4 3.3 %collective-permute-done.29.refs_30_ = bf16[344,256]{1,0:T(8,128)(2,1)S(1)} collective-permute-done((bf16[344,256]{1,0:T(8,128)(2,1)S(1)}, bf16[344,256]{1,0:T(8,128)(2,1)S(1)}, u32[]{:S(2)}, u32[]{:S(2)}) %collective-permute-start.29) | collective-permute-done | bytes 176160 | tf_op jit(solution)/shard_map/ppermute | solution.py:132
  44.7 1.0 %copy-done.2 = bf16[512,512]{1,0:T(8,128)(2,1)S(1)} copy-done((bf16[512,512]{1,0:T(8,128)(2,1)S(1)}, bf16[512,512]{1,0:T(8,128)(2,1)}, u32[]{:S(2)}) %copy-start.2) | copy-done | bytes 524312
  45.7 0.9 %copy-done.3 = f32[256,128]{1,0:T(8,128)S(1)} copy-done((f32[256,128]{1,0:T(8,128)S(1)}, f32[256,128]{1,0:T(8,128)}, u32[]{:S(2)}) %copy-start.3) | copy-done | bytes 131096
  46.6 0.7 copy-done.4
  47.3 1.3 %stage.1 = (bf16[1536,384]{1,0:T(8,128)(2,1)S(1)}, bf16[512,512]{1,0:T(8,128)(2,1)S(1)}, f32[1536]{0:T(1024)S(1)}, f32[256,128]{1,0:T(8,128)S(1)}) custom-call(bf16[1536,3072]{1,0:T(8,128)(2,1)} %w_query_hbm.1, bf16[512,512]{1,0:T(8,128)(2,1)S(1)} %copy-done.2, f32[1536]{0:T(1024)S(1)} %copy-done.4, f32[256,128]{1,0:T(8,128)S(1)} %copy-done.3), custom_call_target="tpu_custom_call" | custom-call | tf_op jit(solution)/shard_map/stage/pallas_call | solution.py:253
  48.7 5.8 %attend.1.refs_0_ = bf16[256,256]{1,0:T(8,128)(2,1)S(1)} custom-call(bf16[344,256]{1,0:T(8,128)(2,1)S(1)} %copy-done.1, bf16[344,256]{1,0:T(8,128)(2,1)S(1)} %collective-permute-done.refs_1_, bf16[344,256]{1,0:T(8,128)(2,1)S(1)} %collective-permute-done.1.refs_2_, bf16[344,256]{1,0:T(8,128)(2,1)S(1)} %collective-permute-done.2.refs_3_, ...), custom_call_target="tpu_custom_call" | custom-call | tf_op jit(solution)/shard_map/attend/pallas_call | solution.py:417
  54.5 3.3 %collective-permute-start.34 = (bf16[256,256]{1,0:T(8,128)(2,1)S(1)}, bf16[256,256]{1,0:T(8,128)(2,1)S(1)}, u32[]{:S(2)}, u32[]{:S(2)}) collective-permute-start(bf16[256,256]{1,0:T(8,128)(2,1)S(1)} %attend.1.refs_0_), channel_id=1, source_target_pairs={{0,16},{4,20},{8,24},{12,28},{16,0},{20,4},{24,8},{28,12},{1,17},{... | collective-permute-start | bytes 393224 | tf_op jit(solution)/shard_map/ppermute | solution.py:132
  57.8 1.2 %collective-permute-start.31 = (bf16[256,256]{1,0:T(8,128)(2,1)S(1)}, bf16[256,256]{1,0:T(8,128)(2,1)S(1)}, u32[]{:S(2)}, u32[]{:S(2)}) collective-permute-start(bf16[256,256]{1,0:T(8,128)(2,1)S(1)} %attend.1.refs_0_), channel_id=1, source_target_pairs={{0,4},{4,0},{8,12},{12,8},{16,20},{20,16},{24,28},{28,24},{1,5},{5... | collective-permute-start | bytes 393224 | tf_op jit(solution)/shard_map/ppermute | solution.py:132
  59.1 1.7 %collective-permute-start.32 = (bf16[256,256]{1,0:T(8,128)(2,1)S(1)}, bf16[256,256]{1,0:T(8,128)(2,1)S(1)}, u32[]{:S(2)}, u32[]{:S(2)}) collective-permute-start(bf16[256,256]{1,0:T(8,128)(2,1)S(1)} %attend.1.refs_0_), channel_id=1, source_target_pairs={{0,8},{4,12},{8,0},{12,4},{16,24},{20,28},{24,16},{28,20},{1,9},{5... | collective-permute-start | bytes 393224 | tf_op jit(solution)/shard_map/ppermute | solution.py:132
  60.7 4.2 %collective-permute-done.34.refs_4_ = bf16[256,256]{1,0:T(8,128)(2,1)S(1)} collective-permute-done((bf16[256,256]{1,0:T(8,128)(2,1)S(1)}, bf16[256,256]{1,0:T(8,128)(2,1)S(1)}, u32[]{:S(2)}, u32[]{:S(2)}) %collective-permute-start.34) | collective-permute-done | bytes 131104 | tf_op jit(solution)/shard_map/ppermute | solution.py:132
  64.9 1.3 %collective-permute-start.37 = (bf16[256,256]{1,0:T(8,128)(2,1)S(1)}, bf16[256,256]{1,0:T(8,128)(2,1)S(1)}, u32[]{:S(2)}, u32[]{:S(2)}) collective-permute-start(bf16[256,256]{1,0:T(8,128)(2,1)S(1)} %collective-permute-done.34.refs_4_), channel_id=1, source_target_pairs={{0,12},{4,8},{8,4},{12,0},{16,28},{20,24},{24,20},{28,16},{1,13},{... | collective-permute-start | bytes 393224 | tf_op jit(solution)/shard_map/ppermute | solution.py:132
  66.2 1.4 %collective-permute-start.36 = (bf16[256,256]{1,0:T(8,128)(2,1)S(1)}, bf16[256,256]{1,0:T(8,128)(2,1)S(1)}, u32[]{:S(2)}, u32[]{:S(2)}) collective-permute-start(bf16[256,256]{1,0:T(8,128)(2,1)S(1)} %collective-permute-done.34.refs_4_), channel_id=1, source_target_pairs={{0,8},{4,12},{8,0},{12,4},{16,24},{20,28},{24,16},{28,20},{1,9},{5... | collective-permute-start | bytes 393224 | tf_op jit(solution)/shard_map/ppermute | solution.py:132
  67.6 0.8 collective-permute-start.35
  68.8 3.4 %collective-permute-done.37.refs_7_ = bf16[256,256]{1,0:T(8,128)(2,1)S(1)} collective-permute-done((bf16[256,256]{1,0:T(8,128)(2,1)S(1)}, bf16[256,256]{1,0:T(8,128)(2,1)S(1)}, u32[]{:S(2)}, u32[]{:S(2)}) %collective-permute-start.37) | collective-permute-done | bytes 131104 | tf_op jit(solution)/shard_map/ppermute | solution.py:132
  72.2 2.6 %collective-permute-done.36.refs_6_ = bf16[256,256]{1,0:T(8,128)(2,1)S(1)} collective-permute-done((bf16[256,256]{1,0:T(8,128)(2,1)S(1)}, bf16[256,256]{1,0:T(8,128)(2,1)S(1)}, u32[]{:S(2)}, u32[]{:S(2)}) %collective-permute-start.36) | collective-permute-done | bytes 131104 | tf_op jit(solution)/shard_map/ppermute | solution.py:132
  74.8 1.7 %collective-permute-done.33.refs_3_ = bf16[256,256]{1,0:T(8,128)(2,1)S(1)} collective-permute-done((bf16[256,256]{1,0:T(8,128)(2,1)S(1)}, bf16[256,256]{1,0:T(8,128)(2,1)S(1)}, u32[]{:S(2)}, u32[]{:S(2)}) %collective-permute-start.33) | collective-permute-done | bytes 131104 | tf_op jit(solution)/shard_map/ppermute | solution.py:132
  76.5 1.3 %project_out.1 = (f32[64,896]{1,0:T(8,128)S(1)}, bf16[64,896]{1,0:T(8,128)(2,1)S(1)}, bf16[64,896]{1,0:T(8,128)(2,1)S(1)}, bf16[64,896]{1,0:T(8,128)(2,1)S(1)}) custom-call(bf16[256,256]{1,0:T(8,128)(2,1)S(1)} %attend.1.refs_0_, bf16[256,256]{1,0:T(8,128)(2,1)S(1)} %collective-permute-done.31.refs_1_, bf16[256,256]{1,0:T(8,128)(2,1)S(1)} %collective-permute-done.32.refs_2_, ...), custom_call_target="tpu_custom_call" | custom-call | tf_op jit(solution)/shard_map/project_out/pallas_call | solution.py:468
  77.9 1.3 %collective-permute-start.39 = (bf16[64,896]{1,0:T(8,128)(2,1)S(1)}, bf16[64,896]{1,0:T(8,128)(2,1)S(1)}, u32[]{:S(2)}, u32[]{:S(2)}) collective-permute-start(bf16[64,896]{1,0:T(8,128)(2,1)S(1)} %get-tuple-element.19), channel_id=1, source_target_pairs={{0,2},{1,3},{2,0},{3,1},{4,6},{5,7},{6,4},{7,5},{8,10},{9,11},{10,... | collective-permute-start | bytes 344072 | tf_op jit(solution)/shard_map/ppermute | solution.py:132
  79.2 0.6 collective-permute-start.40
  79.7 4.2 %collective-permute-done.39 = bf16[64,896]{1,0:T(8,128)(2,1)S(1)} collective-permute-done((bf16[64,896]{1,0:T(8,128)(2,1)S(1)}, bf16[64,896]{1,0:T(8,128)(2,1)S(1)}, u32[]{:S(2)}, u32[]{:S(2)}) %collective-permute-start.39) | collective-permute-done | bytes 114720 | tf_op jit(solution)/shard_map/ppermute | solution.py:132
  84.0 1.4 %collective-permute-done.40 = bf16[64,896]{1,0:T(8,128)(2,1)S(1)} collective-permute-done((bf16[64,896]{1,0:T(8,128)(2,1)S(1)}, bf16[64,896]{1,0:T(8,128)(2,1)S(1)}, u32[]{:S(2)}, u32[]{:S(2)}) %collective-permute-start.40) | collective-permute-done | bytes 114720 | tf_op jit(solution)/shard_map/ppermute | solution.py:132
  85.3 0.7 add_convert_fusion
  (49 shorter events, 1.2 us)
Async XLA Ops:
  1.9 46.8 %copy-start.1 = (bf16[344,256]{1,0:T(8,128)(2,1)S(1)}, bf16[344,256]{1,0:T(8,128)(2,1)}, u32[]{:S(2)}) copy-start(bf16[344,256]{1,0:T(8,128)(2,1)} %pack.1.refs_0_) | copy-start | bytes 528388
  1.9 12.7 %collective-permute-start.15 = (bf16[344,256]{1,0:T(8,128)(2,1)}, bf16[344,256]{1,0:T(8,128)(2,1)S(1)}, u32[]{:S(2)}, u32[]{:S(2)}) collective-permute-start(bf16[344,256]{1,0:T(8,128)(2,1)} %pack.1.refs_0_), channel_id=1, source_target_pairs={{0,16},{4,20},{8,24},{12,28},{16,0},{20,4},{24,8},{28,12},{1,17},{... | collective-permute-start | bytes 528392 | tf_op jit(solution)/shard_map/ppermute | solution.py:132
  6.0 9.3 %collective-permute-start.7 = (bf16[344,256]{1,0:T(8,128)(2,1)}, bf16[344,256]{1,0:T(8,128)(2,1)S(1)}, u32[]{:S(2)}, u32[]{:S(2)}) collective-permute-start(bf16[344,256]{1,0:T(8,128)(2,1)} %pack.1.refs_0_), channel_id=1, source_target_pairs={{0,8},{4,12},{8,0},{12,4},{16,24},{20,28},{24,16},{28,20},{1,9},{5... | collective-permute-start | bytes 528392 | tf_op jit(solution)/shard_map/ppermute | solution.py:132
  7.6 9.2 %collective-permute-start.3 = (bf16[344,256]{1,0:T(8,128)(2,1)}, bf16[344,256]{1,0:T(8,128)(2,1)S(1)}, u32[]{:S(2)}, u32[]{:S(2)}) collective-permute-start(bf16[344,256]{1,0:T(8,128)(2,1)} %pack.1.refs_0_), channel_id=1, source_target_pairs={{0,4},{4,0},{8,12},{12,8},{16,20},{20,16},{24,28},{28,24},{1,5},{5... | collective-permute-start | bytes 528392 | tf_op jit(solution)/shard_map/ppermute | solution.py:132
  9.1 9.2 %collective-permute-start.1 = (bf16[344,256]{1,0:T(8,128)(2,1)}, bf16[344,256]{1,0:T(8,128)(2,1)S(1)}, u32[]{:S(2)}, u32[]{:S(2)}) collective-permute-start(bf16[344,256]{1,0:T(8,128)(2,1)} %pack.1.refs_0_), channel_id=1, source_target_pairs={{0,2},{1,3},{2,0},{3,1},{4,6},{5,7},{6,4},{7,5},{8,10},{9,11},{10,... | collective-permute-start | bytes 528392 | tf_op jit(solution)/shard_map/ppermute | solution.py:132
  10.6 7.7 %collective-permute-start = (bf16[344,256]{1,0:T(8,128)(2,1)}, bf16[344,256]{1,0:T(8,128)(2,1)S(1)}, u32[]{:S(2)}, u32[]{:S(2)}) collective-permute-start(bf16[344,256]{1,0:T(8,128)(2,1)} %pack.1.refs_0_), channel_id=1, source_target_pairs={{0,1},{1,0},{2,3},{3,2},{4,5},{5,4},{6,7},{7,6},{8,9},{9,8},{10,11... | collective-permute-start | bytes 528392 | tf_op jit(solution)/shard_map/ppermute | solution.py:132
  14.6 5.5 %collective-permute-start.23 = (bf16[344,256]{1,0:T(8,128)(2,1)S(1)}, bf16[344,256]{1,0:T(8,128)(2,1)S(1)}, u32[]{:S(2)}, u32[]{:S(2)}) collective-permute-start(bf16[344,256]{1,0:T(8,128)(2,1)S(1)} %collective-permute-done.15.refs_16_), channel_id=1, source_target_pairs={{0,8},{4,12},{8,0},{12,4},{16,24},{20,28},{24,16},{28,20},{1,9},{5... | collective-permute-start | bytes 528392 | tf_op jit(solution)/shard_map/ppermute | solution.py:132
  15.3 6.3 %collective-permute-start.19 = (bf16[344,256]{1,0:T(8,128)(2,1)S(1)}, bf16[344,256]{1,0:T(8,128)(2,1)S(1)}, u32[]{:S(2)}, u32[]{:S(2)}) collective-permute-start(bf16[344,256]{1,0:T(8,128)(2,1)S(1)} %collective-permute-done.15.refs_16_), channel_id=1, source_target_pairs={{0,4},{4,0},{8,12},{12,8},{16,20},{20,16},{24,28},{28,24},{1,5},{5... | collective-permute-start | bytes 528392 | tf_op jit(solution)/shard_map/ppermute | solution.py:132
  16.8 6.8 %collective-permute-start.17 = (bf16[344,256]{1,0:T(8,128)(2,1)S(1)}, bf16[344,256]{1,0:T(8,128)(2,1)S(1)}, u32[]{:S(2)}, u32[]{:S(2)}) collective-permute-start(bf16[344,256]{1,0:T(8,128)(2,1)S(1)} %collective-permute-done.15.refs_16_), channel_id=1, source_target_pairs={{0,2},{1,3},{2,0},{3,1},{4,6},{5,7},{6,4},{7,5},{8,10},{9,11},{10,... | collective-permute-start | bytes 528392 | tf_op jit(solution)/shard_map/ppermute | solution.py:132
  18.3 7.3 %collective-permute-start.16 = (bf16[344,256]{1,0:T(8,128)(2,1)S(1)}, bf16[344,256]{1,0:T(8,128)(2,1)S(1)}, u32[]{:S(2)}, u32[]{:S(2)}) collective-permute-start(bf16[344,256]{1,0:T(8,128)(2,1)S(1)} %collective-permute-done.15.refs_16_), channel_id=1, source_target_pairs={{0,1},{1,0},{2,3},{3,2},{4,5},{5,4},{6,7},{7,6},{8,9},{9,8},{10,11... | collective-permute-start | bytes 528392 | tf_op jit(solution)/shard_map/ppermute | solution.py:132
  18.3 7.3 %collective-permute-start.11 = (bf16[344,256]{1,0:T(8,128)(2,1)S(1)}, bf16[344,256]{1,0:T(8,128)(2,1)S(1)}, u32[]{:S(2)}, u32[]{:S(2)}) collective-permute-start(bf16[344,256]{1,0:T(8,128)(2,1)S(1)} %collective-permute-done.7.refs_8_), channel_id=1, source_target_pairs={{0,4},{4,0},{8,12},{12,8},{16,20},{20,16},{24,28},{28,24},{1,5},{5... | collective-permute-start | bytes 528392 | tf_op jit(solution)/shard_map/ppermute | solution.py:132
  20.1 7.3 %collective-permute-start.9 = (bf16[344,256]{1,0:T(8,128)(2,1)S(1)}, bf16[344,256]{1,0:T(8,128)(2,1)S(1)}, u32[]{:S(2)}, u32[]{:S(2)}) collective-permute-start(bf16[344,256]{1,0:T(8,128)(2,1)S(1)} %collective-permute-done.7.refs_8_), channel_id=1, source_target_pairs={{0,2},{1,3},{2,0},{3,1},{4,6},{5,7},{6,4},{7,5},{8,10},{9,11},{10,... | collective-permute-start | bytes 528392 | tf_op jit(solution)/shard_map/ppermute | solution.py:132
  21.6 5.8 %collective-permute-start.8 = (bf16[344,256]{1,0:T(8,128)(2,1)S(1)}, bf16[344,256]{1,0:T(8,128)(2,1)S(1)}, u32[]{:S(2)}, u32[]{:S(2)}) collective-permute-start(bf16[344,256]{1,0:T(8,128)(2,1)S(1)} %collective-permute-done.7.refs_8_), channel_id=1, source_target_pairs={{0,1},{1,0},{2,3},{3,2},{4,5},{5,4},{6,7},{7,6},{8,9},{9,8},{10,11... | collective-permute-start | bytes 528392 | tf_op jit(solution)/shard_map/ppermute | solution.py:132
  23.6 7.3 %collective-permute-start.5 = (bf16[344,256]{1,0:T(8,128)(2,1)S(1)}, bf16[344,256]{1,0:T(8,128)(2,1)S(1)}, u32[]{:S(2)}, u32[]{:S(2)}) collective-permute-start(bf16[344,256]{1,0:T(8,128)(2,1)S(1)} %collective-permute-done.3.refs_4_), channel_id=1, source_target_pairs={{0,2},{1,3},{2,0},{3,1},{4,6},{5,7},{6,4},{7,5},{8,10},{9,11},{10,... | collective-permute-start | bytes 528392 | tf_op jit(solution)/shard_map/ppermute | solution.py:132
  25.7 5.2 %collective-permute-start.4 = (bf16[344,256]{1,0:T(8,128)(2,1)S(1)}, bf16[344,256]{1,0:T(8,128)(2,1)S(1)}, u32[]{:S(2)}, u32[]{:S(2)}) collective-permute-start(bf16[344,256]{1,0:T(8,128)(2,1)S(1)} %collective-permute-done.3.refs_4_), channel_id=1, source_target_pairs={{0,1},{1,0},{2,3},{3,2},{4,5},{5,4},{6,7},{7,6},{8,9},{9,8},{10,11... | collective-permute-start | bytes 528392 | tf_op jit(solution)/shard_map/ppermute | solution.py:132
  25.7 6.7 %collective-permute-start.2 = (bf16[344,256]{1,0:T(8,128)(2,1)S(1)}, bf16[344,256]{1,0:T(8,128)(2,1)S(1)}, u32[]{:S(2)}, u32[]{:S(2)}) collective-permute-start(bf16[344,256]{1,0:T(8,128)(2,1)S(1)} %collective-permute-done.1.refs_2_), channel_id=1, source_target_pairs={{0,1},{1,0},{2,3},{3,2},{4,5},{5,4},{6,7},{7,6},{8,9},{9,8},{10,11... | collective-permute-start | bytes 528392 | tf_op jit(solution)/shard_map/ppermute | solution.py:132
  27.4 5.5 %collective-permute-start.27 = (bf16[344,256]{1,0:T(8,128)(2,1)S(1)}, bf16[344,256]{1,0:T(8,128)(2,1)S(1)}, u32[]{:S(2)}, u32[]{:S(2)}) collective-permute-start(bf16[344,256]{1,0:T(8,128)(2,1)S(1)} %collective-permute-done.23.refs_24_), channel_id=1, source_target_pairs={{0,4},{4,0},{8,12},{12,8},{16,20},{20,16},{24,28},{28,24},{1,5},{5... | collective-permute-start | bytes 528392 | tf_op jit(solution)/shard_map/ppermute | solution.py:132
  27.5 6.5 %collective-permute-start.25 = (bf16[344,256]{1,0:T(8,128)(2,1)S(1)}, bf16[344,256]{1,0:T(8,128)(2,1)S(1)}, u32[]{:S(2)}, u32[]{:S(2)}) collective-permute-start(bf16[344,256]{1,0:T(8,128)(2,1)S(1)} %collective-permute-done.23.refs_24_), channel_id=1, source_target_pairs={{0,2},{1,3},{2,0},{3,1},{4,6},{5,7},{6,4},{7,5},{8,10},{9,11},{10,... | collective-permute-start | bytes 528392 | tf_op jit(solution)/shard_map/ppermute | solution.py:132
  30.8 3.1 %collective-permute-start.24 = (bf16[344,256]{1,0:T(8,128)(2,1)S(1)}, bf16[344,256]{1,0:T(8,128)(2,1)S(1)}, u32[]{:S(2)}, u32[]{:S(2)}) collective-permute-start(bf16[344,256]{1,0:T(8,128)(2,1)S(1)} %collective-permute-done.23.refs_24_), channel_id=1, source_target_pairs={{0,1},{1,0},{2,3},{3,2},{4,5},{5,4},{6,7},{7,6},{8,9},{9,8},{10,11... | collective-permute-start | bytes 528392 | tf_op jit(solution)/shard_map/ppermute | solution.py:132
  30.9 6.9 %collective-permute-start.21 = (bf16[344,256]{1,0:T(8,128)(2,1)S(1)}, bf16[344,256]{1,0:T(8,128)(2,1)S(1)}, u32[]{:S(2)}, u32[]{:S(2)}) collective-permute-start(bf16[344,256]{1,0:T(8,128)(2,1)S(1)} %collective-permute-done.19.refs_20_), channel_id=1, source_target_pairs={{0,2},{1,3},{2,0},{3,1},{4,6},{5,7},{6,4},{7,5},{8,10},{9,11},{10,... | collective-permute-start | bytes 528392 | tf_op jit(solution)/shard_map/ppermute | solution.py:132
  32.4 5.4 %collective-permute-start.20 = (bf16[344,256]{1,0:T(8,128)(2,1)S(1)}, bf16[344,256]{1,0:T(8,128)(2,1)S(1)}, u32[]{:S(2)}, u32[]{:S(2)}) collective-permute-start(bf16[344,256]{1,0:T(8,128)(2,1)S(1)} %collective-permute-done.19.refs_20_), channel_id=1, source_target_pairs={{0,1},{1,0},{2,3},{3,2},{4,5},{5,4},{6,7},{7,6},{8,9},{9,8},{10,11... | collective-permute-start | bytes 528392 | tf_op jit(solution)/shard_map/ppermute | solution.py:132
  32.9 5.4 %collective-permute-start.18 = (bf16[344,256]{1,0:T(8,128)(2,1)S(1)}, bf16[344,256]{1,0:T(8,128)(2,1)S(1)}, u32[]{:S(2)}, u32[]{:S(2)}) collective-permute-start(bf16[344,256]{1,0:T(8,128)(2,1)S(1)} %collective-permute-done.17.refs_18_), channel_id=1, source_target_pairs={{0,1},{1,0},{2,3},{3,2},{4,5},{5,4},{6,7},{7,6},{8,9},{9,8},{10,11... | collective-permute-start | bytes 528392 | tf_op jit(solution)/shard_map/ppermute | solution.py:132
  34.0 5.3 %collective-permute-start.12 = (bf16[344,256]{1,0:T(8,128)(2,1)S(1)}, bf16[344,256]{1,0:T(8,128)(2,1)S(1)}, u32[]{:S(2)}, u32[]{:S(2)}) collective-permute-start(bf16[344,256]{1,0:T(8,128)(2,1)S(1)} %collective-permute-done.11.refs_12_), channel_id=1, source_target_pairs={{0,1},{1,0},{2,3},{3,2},{4,5},{5,4},{6,7},{7,6},{8,9},{9,8},{10,11... | collective-permute-start | bytes 528392 | tf_op jit(solution)/shard_map/ppermute | solution.py:132
  34.0 6.9 %collective-permute-start.13 = (bf16[344,256]{1,0:T(8,128)(2,1)S(1)}, bf16[344,256]{1,0:T(8,128)(2,1)S(1)}, u32[]{:S(2)}, u32[]{:S(2)}) collective-permute-start(bf16[344,256]{1,0:T(8,128)(2,1)S(1)} %collective-permute-done.9.refs_10_), channel_id=1, source_target_pairs={{0,4},{4,0},{8,12},{12,8},{16,20},{20,16},{24,28},{28,24},{1,5},{5... | collective-permute-start | bytes 528392 | tf_op jit(solution)/shard_map/ppermute | solution.py:132
  37.7 3.1 %collective-permute-start.10 = (bf16[344,256]{1,0:T(8,128)(2,1)S(1)}, bf16[344,256]{1,0:T(8,128)(2,1)S(1)}, u32[]{:S(2)}, u32[]{:S(2)}) collective-permute-start(bf16[344,256]{1,0:T(8,128)(2,1)S(1)} %collective-permute-done.9.refs_10_), channel_id=1, source_target_pairs={{0,1},{1,0},{2,3},{3,2},{4,5},{5,4},{6,7},{7,6},{8,9},{9,8},{10,11... | collective-permute-start | bytes 528392 | tf_op jit(solution)/shard_map/ppermute | solution.py:132
  37.7 3.6 %collective-permute-start.6 = (bf16[344,256]{1,0:T(8,128)(2,1)S(1)}, bf16[344,256]{1,0:T(8,128)(2,1)S(1)}, u32[]{:S(2)}, u32[]{:S(2)}) collective-permute-start(bf16[344,256]{1,0:T(8,128)(2,1)S(1)} %collective-permute-done.5.refs_6_), channel_id=1, source_target_pairs={{0,1},{1,0},{2,3},{3,2},{4,5},{5,4},{6,7},{7,6},{8,9},{9,8},{10,11... | collective-permute-start | bytes 528392 | tf_op jit(solution)/shard_map/ppermute | solution.py:132
  38.2 6.4 %collective-permute-start.29 = (bf16[344,256]{1,0:T(8,128)(2,1)S(1)}, bf16[344,256]{1,0:T(8,128)(2,1)S(1)}, u32[]{:S(2)}, u32[]{:S(2)}) collective-permute-start(bf16[344,256]{1,0:T(8,128)(2,1)S(1)} %collective-permute-done.25.refs_26_), channel_id=1, source_target_pairs={{0,4},{4,0},{8,12},{12,8},{16,20},{20,16},{24,28},{28,24},{1,5},{5... | collective-permute-start | bytes 528392 | tf_op jit(solution)/shard_map/ppermute | solution.py:132
  39.2 9.4 %collective-permute-start.26 = (bf16[344,256]{1,0:T(8,128)(2,1)S(1)}, bf16[344,256]{1,0:T(8,128)(2,1)S(1)}, u32[]{:S(2)}, u32[]{:S(2)}) collective-permute-start(bf16[344,256]{1,0:T(8,128)(2,1)S(1)} %collective-permute-done.25.refs_26_), channel_id=1, source_target_pairs={{0,1},{1,0},{2,3},{3,2},{4,5},{5,4},{6,7},{7,6},{8,9},{9,8},{10,11... | collective-permute-start | bytes 528392 | tf_op jit(solution)/shard_map/ppermute | solution.py:132
  40.8 7.8 %collective-permute-start.28 = (bf16[344,256]{1,0:T(8,128)(2,1)S(1)}, bf16[344,256]{1,0:T(8,128)(2,1)S(1)}, u32[]{:S(2)}, u32[]{:S(2)}) collective-permute-start(bf16[344,256]{1,0:T(8,128)(2,1)S(1)} %collective-permute-done.27.refs_28_), channel_id=1, source_target_pairs={{0,1},{1,0},{2,3},{3,2},{4,5},{5,4},{6,7},{7,6},{8,9},{9,8},{10,11... | collective-permute-start | bytes 528392 | tf_op jit(solution)/shard_map/ppermute | solution.py:132
  40.8 7.8 %collective-permute-start.22 = (bf16[344,256]{1,0:T(8,128)(2,1)S(1)}, bf16[344,256]{1,0:T(8,128)(2,1)S(1)}, u32[]{:S(2)}, u32[]{:S(2)}) collective-permute-start(bf16[344,256]{1,0:T(8,128)(2,1)S(1)} %collective-permute-done.21.refs_22_), channel_id=1, source_target_pairs={{0,1},{1,0},{2,3},{3,2},{4,5},{5,4},{6,7},{7,6},{8,9},{9,8},{10,11... | collective-permute-start | bytes 528392 | tf_op jit(solution)/shard_map/ppermute | solution.py:132
  41.4 7.3 %collective-permute-start.14 = (bf16[344,256]{1,0:T(8,128)(2,1)S(1)}, bf16[344,256]{1,0:T(8,128)(2,1)S(1)}, u32[]{:S(2)}, u32[]{:S(2)}) collective-permute-start(bf16[344,256]{1,0:T(8,128)(2,1)S(1)} %collective-permute-done.13.refs_14_), channel_id=1, source_target_pairs={{0,1},{1,0},{2,3},{3,2},{4,5},{5,4},{6,7},{7,6},{8,9},{9,8},{10,11... | collective-permute-start | bytes 528392 | tf_op jit(solution)/shard_map/ppermute | solution.py:132
  44.7 4.0 %collective-permute-start.30 = (bf16[344,256]{1,0:T(8,128)(2,1)S(1)}, bf16[344,256]{1,0:T(8,128)(2,1)S(1)}, u32[]{:S(2)}, u32[]{:S(2)}) collective-permute-start(bf16[344,256]{1,0:T(8,128)(2,1)S(1)} %collective-permute-done.29.refs_30_), channel_id=1, source_target_pairs={{0,1},{1,0},{2,3},{3,2},{4,5},{5,4},{6,7},{7,6},{8,9},{9,8},{10,11... | collective-permute-start | bytes 528392 | tf_op jit(solution)/shard_map/ppermute | solution.py:132
  44.7 1.0 %copy-start.2 = (bf16[512,512]{1,0:T(8,128)(2,1)S(1)}, bf16[512,512]{1,0:T(8,128)(2,1)}, u32[]{:S(2)}) copy-start(bf16[512,512]{1,0:T(8,128)(2,1)} %w_kv_hbm.1) | copy-start | bytes 1572868
  45.7 0.9 %copy-start.3 = (f32[256,128]{1,0:T(8,128)S(1)}, f32[256,128]{1,0:T(8,128)}, u32[]{:S(2)}) copy-start(f32[256,128]{1,0:T(8,128)} %constant.2.clone.turn_hbm) | copy-start | bytes 393220
  46.6 0.7 copy-start.4
  48.7 27.8 %copy-start = (bf16[2048,896]{1,0:T(8,128)(2,1)S(1)}, bf16[2048,896]{1,0:T(8,128)(2,1)}, u32[]{:S(2)}) copy-start(bf16[2048,896]{1,0:T(8,128)(2,1)} %refs_8_.1) | copy-start | bytes 11010052
  54.5 10.4 %collective-permute-start.34 = (bf16[256,256]{1,0:T(8,128)(2,1)S(1)}, bf16[256,256]{1,0:T(8,128)(2,1)S(1)}, u32[]{:S(2)}, u32[]{:S(2)}) collective-permute-start(bf16[256,256]{1,0:T(8,128)(2,1)S(1)} %attend.1.refs_0_), channel_id=1, source_target_pairs={{0,16},{4,20},{8,24},{12,28},{16,0},{20,4},{24,8},{28,12},{1,17},{... | collective-permute-start | bytes 393224 | tf_op jit(solution)/shard_map/ppermute | solution.py:132
  57.8 10.6 %collective-permute-start.31 = (bf16[256,256]{1,0:T(8,128)(2,1)S(1)}, bf16[256,256]{1,0:T(8,128)(2,1)S(1)}, u32[]{:S(2)}, u32[]{:S(2)}) collective-permute-start(bf16[256,256]{1,0:T(8,128)(2,1)S(1)} %attend.1.refs_0_), channel_id=1, source_target_pairs={{0,4},{4,0},{8,12},{12,8},{16,20},{20,16},{24,28},{28,24},{1,5},{5... | collective-permute-start | bytes 393224 | tf_op jit(solution)/shard_map/ppermute | solution.py:132
  59.1 9.7 %collective-permute-start.32 = (bf16[256,256]{1,0:T(8,128)(2,1)S(1)}, bf16[256,256]{1,0:T(8,128)(2,1)S(1)}, u32[]{:S(2)}, u32[]{:S(2)}) collective-permute-start(bf16[256,256]{1,0:T(8,128)(2,1)S(1)} %attend.1.refs_0_), channel_id=1, source_target_pairs={{0,8},{4,12},{8,0},{12,4},{16,24},{20,28},{24,16},{28,20},{1,9},{5... | collective-permute-start | bytes 393224 | tf_op jit(solution)/shard_map/ppermute | solution.py:132
  64.9 7.3 %collective-permute-start.37 = (bf16[256,256]{1,0:T(8,128)(2,1)S(1)}, bf16[256,256]{1,0:T(8,128)(2,1)S(1)}, u32[]{:S(2)}, u32[]{:S(2)}) collective-permute-start(bf16[256,256]{1,0:T(8,128)(2,1)S(1)} %collective-permute-done.34.refs_4_), channel_id=1, source_target_pairs={{0,12},{4,8},{8,4},{12,0},{16,28},{20,24},{24,20},{28,16},{1,13},{... | collective-permute-start | bytes 393224 | tf_op jit(solution)/shard_map/ppermute | solution.py:132
  66.2 8.5 %collective-permute-start.36 = (bf16[256,256]{1,0:T(8,128)(2,1)S(1)}, bf16[256,256]{1,0:T(8,128)(2,1)S(1)}, u32[]{:S(2)}, u32[]{:S(2)}) collective-permute-start(bf16[256,256]{1,0:T(8,128)(2,1)S(1)} %collective-permute-done.34.refs_4_), channel_id=1, source_target_pairs={{0,8},{4,12},{8,0},{12,4},{16,24},{20,28},{24,16},{28,20},{1,9},{5... | collective-permute-start | bytes 393224 | tf_op jit(solution)/shard_map/ppermute | solution.py:132
  67.6 7.2 %collective-permute-start.35 = (bf16[256,256]{1,0:T(8,128)(2,1)S(1)}, bf16[256,256]{1,0:T(8,128)(2,1)S(1)}, u32[]{:S(2)}, u32[]{:S(2)}) collective-permute-start(bf16[256,256]{1,0:T(8,128)(2,1)S(1)} %collective-permute-done.34.refs_4_), channel_id=1, source_target_pairs={{0,4},{4,0},{8,12},{12,8},{16,20},{20,16},{24,28},{28,24},{1,5},{5... | collective-permute-start | bytes 393224 | tf_op jit(solution)/shard_map/ppermute | solution.py:132
  68.4 8.1 %collective-permute-start.33 = (bf16[256,256]{1,0:T(8,128)(2,1)S(1)}, bf16[256,256]{1,0:T(8,128)(2,1)S(1)}, u32[]{:S(2)}, u32[]{:S(2)}) collective-permute-start(bf16[256,256]{1,0:T(8,128)(2,1)S(1)} %collective-permute-done.31.refs_1_), channel_id=1, source_target_pairs={{0,8},{4,12},{8,0},{12,4},{16,24},{20,28},{24,16},{28,20},{1,9},{5... | collective-permute-start | bytes 393224 | tf_op jit(solution)/shard_map/ppermute | solution.py:132
  77.8 1.9 %collective-permute-start.38 = (bf16[64,896]{1,0:T(8,128)(2,1)S(1)}, bf16[64,896]{1,0:T(8,128)(2,1)S(1)}, u32[]{:S(2)}, u32[]{:S(2)}) collective-permute-start(bf16[64,896]{1,0:T(8,128)(2,1)S(1)} %get-tuple-element.18), channel_id=1, source_target_pairs={{0,1},{1,0},{2,3},{3,2},{4,5},{5,4},{6,7},{7,6},{8,9},{9,8},{10,11... | collective-permute-start | bytes 344072 | tf_op jit(solution)/shard_map/ppermute | solution.py:132
  77.9 6.1 %collective-permute-start.39 = (bf16[64,896]{1,0:T(8,128)(2,1)S(1)}, bf16[64,896]{1,0:T(8,128)(2,1)S(1)}, u32[]{:S(2)}, u32[]{:S(2)}) collective-permute-start(bf16[64,896]{1,0:T(8,128)(2,1)S(1)} %get-tuple-element.19), channel_id=1, source_target_pairs={{0,2},{1,3},{2,0},{3,1},{4,6},{5,7},{6,4},{7,5},{8,10},{9,11},{10,... | collective-permute-start | bytes 344072 | tf_op jit(solution)/shard_map/ppermute | solution.py:132
  79.2 6.2 %collective-permute-start.40 = (bf16[64,896]{1,0:T(8,128)(2,1)S(1)}, bf16[64,896]{1,0:T(8,128)(2,1)S(1)}, u32[]{:S(2)}, u32[]{:S(2)}) collective-permute-start(bf16[64,896]{1,0:T(8,128)(2,1)S(1)} %get-tuple-element.20), channel_id=1, source_target_pairs={{0,3},{1,2},{2,1},{3,0},{4,7},{5,6},{6,5},{7,4},{8,11},{9,10},{10,... | collective-permute-start | bytes 344072 | tf_op jit(solution)/shard_map/ppermute | solution.py:132
where the time goes:
time: 86.3 us; the launch traced here: 86 us
  waiting for transfers between devices  36.4 us (42%)
  starting transfers between devices  35.9 us (42%)
  Pallas kernels  10.3 us (12%)
  local copies, waits for them, and re-layouts  2.65 us (3%)
    ppermute x41, waiting for transfers between devices, exchanged(): return lax.ppermute(x, axes, [(i, i ^ flip) for i in range(devices)])  36.4 us
    ppermute x41, starting transfers between devices, exchanged(): return lax.ppermute(x, axes, [(i, i ^ flip) for i in range(devices)])  35.9 us
    pallas_call x1, Pallas kernels, attend(): pl.pallas_call(functools.partial(attend_kernel, flips, blocks), out_shape...  5.78 us
    unnamed x10, local copies, waits for them, and re-layouts  2.65 us
    pallas_call x1, Pallas kernels, pack(): pl.pallas_call(pack_kernel, out_shape=jax.ShapeDtypeStruct((packed_rows,...  1.89 us
  transfers between devices with their start and end apart: 41, of which 16 were waited for; matrix products, arithmetic and copies ran while one was open for 0% of the time, Pallas kernels for 2%

commit v1 on v0

--- a/solution.py
+++ b/solution.py
@@ -205,21 +205,21 @@
 
 
 HOPS = (
+    ((0, 0), (2, 0)),
     ((0, 0), (4, 0)),
-    ((0, 0), (2, 0)),
     ((0, 0), (1, 0)),
     ((0, 0), (0, 2)),
-    ((1, 0), (0, 2)),
     ((2, 0), (1, 0)),
     ((2, 0), (0, 2)),
-    ((4, 0), (2, 0)),
+    ((1, 0), (0, 2)),
     ((4, 0), (1, 0)),
     ((4, 0), (0, 2)),
+    ((4, 0), (2, 0)),
     ((2, 2), (1, 0)),
-    ((6, 0), (1, 0)),
-    ((6, 0), (0, 2)),
+    ((5, 0), (2, 0)),
+    ((4, 2), (2, 0)),
     ((5, 0), (0, 2)),
-    ((6, 2), (1, 0)),
+    ((6, 0), (1, 2)),
 )
 
 
@@ -479,7 +479,7 @@
     )(*pieces, w_out)
 
 
-SPREAD_HOPS = ((0, 4), (0, 1), (0, 2), (1, 2), (4, 2), (4, 1), (4, 3))
+SPREAD_HOPS = ((0, 4), (0, 2), (0, 1), (2, 1), (4, 2), (4, 1), (4, 3))
 
 
 def rotation_table(blocks, query_rows, key_rows):

time: 86.3 us -> 89.8 us (1.041)
  waiting for transfers between devices: 36.4 us -> 39 us
    ppermute x41, waiting for transfers between devices: 36.4 us -> 39 us  [exchanged(): return lax.ppermute(x, axes, [(i, i ^ flip) for i in range(devices)])]
  transfers between devices with their start and end apart: 41 -> 41, of which waited for: 16 -> 16; matrix products, arithmetic and copies ran while one was open for 0% -> 0% of each run, Pallas kernels for 2% -> 1%
where the time goes in v1:
time: 89.8 us; the launch traced here: 89.5 us
  waiting for transfers between devices  39 us (43%)
  starting transfers between devices  36.7 us (41%)
  Pallas kernels  10.3 us (11%)
  local copies, waits for them, and re-layouts  2.65 us (3%)
    ppermute x41, waiting for transfers between devices, exchanged(): return lax.ppermute(x, axes, [(i, i ^ flip) for i in range(devices)])  39 us
    ppermute x41, starting transfers between devices, exchanged(): return lax.ppermute(x, axes, [(i, i ^ flip) for i in range(devices)])  36.7 us
    pallas_call x1, Pallas kernels, attend(): pl.pallas_call(functools.partial(attend_kernel, flips, blocks), out_shape...  5.8 us
    unnamed x10, local copies, waits for them, and re-layouts  2.65 us
    pallas_call x1, Pallas kernels, pack(): pl.pallas_call(pack_kernel, out_shape=jax.ShapeDtypeStruct((packed_rows,...  1.89 us
  transfers between devices with their start and end apart: 41, of which 16 were waited for; matrix products, arithmetic and copies ran while one was open for 0% of the time, Pallas kernels for 1%

profile of v1, /device:TPU:0, one launch (start us, length us, event | category | flops | bytes accessed | tf_op | source)
XLA Modules:
  0.0 89.5 jit_solution(1335199630994811339)
XLA Ops:
  0.0 1.9 %pack.1.refs_0_ = bf16[344,256]{1,0:T(8,128)(2,1)} custom-call(s32[32]{0:T(128)} %start_hbm.1, f32[1,512]{1,0:T(1,128)} %bitcast.3, bf16[32,384]{1,0:T(8,128)(2,1)} %query_hbm.1, bf16[576,512]{1,0:T(8,128)(2,1)} %bitcast.2), custom_call_target="tpu_custom_call" | custom-call | tf_op jit(solution)/shard_map/pack/pallas_call | solution.py:191
  1.9 4.1 %collective-permute-start.15 = (bf16[344,256]{1,0:T(8,128)(2,1)}, bf16[344,256]{1,0:T(8,128)(2,1)S(1)}, u32[]{:S(2)}, u32[]{:S(2)}) collective-permute-start(bf16[344,256]{1,0:T(8,128)(2,1)} %pack.1.refs_0_), channel_id=1, source_target_pairs={{0,16},{4,20},{8,24},{12,28},{16,0},{20,4},{24,8},{28,12},{1,17},{... | collective-permute-start | bytes 528392 | tf_op jit(solution)/shard_map/ppermute | solution.py:132
  6.0 1.6 %collective-permute-start.7 = (bf16[344,256]{1,0:T(8,128)(2,1)}, bf16[344,256]{1,0:T(8,128)(2,1)S(1)}, u32[]{:S(2)}, u32[]{:S(2)}) collective-permute-start(bf16[344,256]{1,0:T(8,128)(2,1)} %pack.1.refs_0_), channel_id=1, source_target_pairs={{0,8},{4,12},{8,0},{12,4},{16,24},{20,28},{24,16},{28,20},{1,9},{5... | collective-permute-start | bytes 528392 | tf_op jit(solution)/shard_map/ppermute | solution.py:132
  7.6 1.5 %collective-permute-start.3 = (bf16[344,256]{1,0:T(8,128)(2,1)}, bf16[344,256]{1,0:T(8,128)(2,1)S(1)}, u32[]{:S(2)}, u32[]{:S(2)}) collective-permute-start(bf16[344,256]{1,0:T(8,128)(2,1)} %pack.1.refs_0_), channel_id=1, source_target_pairs={{0,4},{4,0},{8,12},{12,8},{16,20},{20,16},{24,28},{28,24},{1,5},{5... | collective-permute-start | bytes 528392 | tf_op jit(solution)/shard_map/ppermute | solution.py:132
  9.1 1.5 %collective-permute-start.1 = (bf16[344,256]{1,0:T(8,128)(2,1)}, bf16[344,256]{1,0:T(8,128)(2,1)S(1)}, u32[]{:S(2)}, u32[]{:S(2)}) collective-permute-start(bf16[344,256]{1,0:T(8,128)(2,1)} %pack.1.refs_0_), channel_id=1, source_target_pairs={{0,2},{1,3},{2,0},{3,1},{4,6},{5,7},{6,4},{7,5},{8,10},{9,11},{10,... | collective-permute-start | bytes 528392 | tf_op jit(solution)/shard_map/ppermute | solution.py:132
  10.6 4.0 %collective-permute-done.15.refs_16_ = bf16[344,256]{1,0:T(8,128)(2,1)S(1)} collective-permute-done((bf16[344,256]{1,0:T(8,128)(2,1)}, bf16[344,256]{1,0:T(8,128)(2,1)S(1)}, u32[]{:S(2)}, u32[]{:S(2)}) %collective-permute-start.15) | collective-permute-done | bytes 176160 | tf_op jit(solution)/shard_map/ppermute | solution.py:132
  14.6 0.7 collective-permute-start.23
  15.3 1.5 %collective-permute-start.19 = (bf16[344,256]{1,0:T(8,128)(2,1)S(1)}, bf16[344,256]{1,0:T(8,128)(2,1)S(1)}, u32[]{:S(2)}, u32[]{:S(2)}) collective-permute-start(bf16[344,256]{1,0:T(8,128)(2,1)S(1)} %collective-permute-done.15.refs_16_), channel_id=1, source_target_pairs={{0,4},{4,0},{8,12},{12,8},{16,20},{20,16},{24,28},{28,24},{1,5},{5... | collective-permute-start | bytes 528392 | tf_op jit(solution)/shard_map/ppermute | solution.py:132
  16.8 1.5 %collective-permute-start.17 = (bf16[344,256]{1,0:T(8,128)(2,1)S(1)}, bf16[344,256]{1,0:T(8,128)(2,1)S(1)}, u32[]{:S(2)}, u32[]{:S(2)}) collective-permute-start(bf16[344,256]{1,0:T(8,128)(2,1)S(1)} %collective-permute-done.15.refs_16_), channel_id=1, source_target_pairs={{0,2},{1,3},{2,0},{3,1},{4,6},{5,7},{6,4},{7,5},{8,10},{9,11},{10,... | collective-permute-start | bytes 528392 | tf_op jit(solution)/shard_map/ppermute | solution.py:132
  18.3 0.6 collective-permute-start.11
  18.9 1.2 %collective-permute-done.23.refs_24_ = bf16[344,256]{1,0:T(8,128)(2,1)S(1)} collective-permute-done((bf16[344,256]{1,0:T(8,128)(2,1)S(1)}, bf16[344,256]{1,0:T(8,128)(2,1)S(1)}, u32[]{:S(2)}, u32[]{:S(2)}) %collective-permute-start.23) | collective-permute-done | bytes 176160 | tf_op jit(solution)/shard_map/ppermute | solution.py:132
  20.1 1.5 %collective-permute-start.9 = (bf16[344,256]{1,0:T(8,128)(2,1)S(1)}, bf16[344,256]{1,0:T(8,128)(2,1)S(1)}, u32[]{:S(2)}, u32[]{:S(2)}) collective-permute-start(bf16[344,256]{1,0:T(8,128)(2,1)S(1)} %collective-permute-done.7.refs_8_), channel_id=1, source_target_pairs={{0,2},{1,3},{2,0},{3,1},{4,6},{5,7},{6,4},{7,5},{8,10},{9,11},{10,... | collective-permute-start | bytes 528392 | tf_op jit(solution)/shard_map/ppermute | solution.py:132
  21.6 2.0 %collective-permute-done.17.refs_18_ = bf16[344,256]{1,0:T(8,128)(2,1)S(1)} collective-permute-done((bf16[344,256]{1,0:T(8,128)(2,1)S(1)}, bf16[344,256]{1,0:T(8,128)(2,1)S(1)}, u32[]{:S(2)}, u32[]{:S(2)}) %collective-permute-start.17) | collective-permute-done | bytes 176160 | tf_op jit(solution)/shard_map/ppermute | solution.py:132
  23.6 2.1 %collective-permute-start.5 = (bf16[344,256]{1,0:T(8,128)(2,1)S(1)}, bf16[344,256]{1,0:T(8,128)(2,1)S(1)}, u32[]{:S(2)}, u32[]{:S(2)}) collective-permute-start(bf16[344,256]{1,0:T(8,128)(2,1)S(1)} %collective-permute-done.3.refs_4_), channel_id=1, source_target_pairs={{0,2},{1,3},{2,0},{3,1},{4,6},{5,7},{6,4},{7,5},{8,10},{9,11},{10,... | collective-permute-start | bytes 528392 | tf_op jit(solution)/shard_map/ppermute | solution.py:132
  25.7 0.5 collective-permute-start.2
  26.2 1.3 %collective-permute-done.9.refs_10_ = bf16[344,256]{1,0:T(8,128)(2,1)S(1)} collective-permute-done((bf16[344,256]{1,0:T(8,128)(2,1)S(1)}, bf16[344,256]{1,0:T(8,128)(2,1)S(1)}, u32[]{:S(2)}, u32[]{:S(2)}) %collective-permute-start.9) | collective-permute-done | bytes 176160 | tf_op jit(solution)/shard_map/ppermute | solution.py:132
  27.4 0.5 collective-permute-start.29
  28.0 6.1 %collective-permute-done.5.refs_6_ = bf16[344,256]{1,0:T(8,128)(2,1)S(1)} collective-permute-done((bf16[344,256]{1,0:T(8,128)(2,1)S(1)}, bf16[344,256]{1,0:T(8,128)(2,1)S(1)}, u32[]{:S(2)}, u32[]{:S(2)}) %collective-permute-start.5) | collective-permute-done | bytes 176160 | tf_op jit(solution)/shard_map/ppermute | solution.py:132
  34.1 1.0 %collective-permute-start.27 = (bf16[344,256]{1,0:T(8,128)(2,1)S(1)}, bf16[344,256]{1,0:T(8,128)(2,1)S(1)}, u32[]{:S(2)}, u32[]{:S(2)}) collective-permute-start(bf16[344,256]{1,0:T(8,128)(2,1)S(1)} %collective-permute-done.19.refs_20_), channel_id=1, source_target_pairs={{0,8},{4,12},{8,0},{12,4},{16,24},{20,28},{24,16},{28,20},{1,9},{5... | collective-permute-start | bytes 528392 | tf_op jit(solution)/shard_map/ppermute | solution.py:132
  35.1 0.6 collective-permute-start.21
  35.7 2.1 %collective-permute-start.25 = (bf16[344,256]{1,0:T(8,128)(2,1)S(1)}, bf16[344,256]{1,0:T(8,128)(2,1)S(1)}, u32[]{:S(2)}, u32[]{:S(2)}) collective-permute-start(bf16[344,256]{1,0:T(8,128)(2,1)S(1)} %collective-permute-done.17.refs_18_), channel_id=1, source_target_pairs={{0,8},{4,12},{8,0},{12,4},{16,24},{20,28},{24,16},{28,20},{1,9},{5... | collective-permute-start | bytes 528392 | tf_op jit(solution)/shard_map/ppermute | solution.py:132
  38.0 2.1 %collective-permute-done.27.refs_28_ = bf16[344,256]{1,0:T(8,128)(2,1)S(1)} collective-permute-done((bf16[344,256]{1,0:T(8,128)(2,1)S(1)}, bf16[344,256]{1,0:T(8,128)(2,1)S(1)}, u32[]{:S(2)}, u32[]{:S(2)}) %collective-permute-start.27) | collective-permute-done | bytes 176160 | tf_op jit(solution)/shard_map/ppermute | solution.py:132
  40.0 0.5 collective-permute-done.21.refs_22_
  40.5 1.2 %collective-permute-start.13 = (bf16[344,256]{1,0:T(8,128)(2,1)S(1)}, bf16[344,256]{1,0:T(8,128)(2,1)S(1)}, u32[]{:S(2)}, u32[]{:S(2)}) collective-permute-start(bf16[344,256]{1,0:T(8,128)(2,1)S(1)} %collective-permute-done.9.refs_10_), channel_id=1, source_target_pairs={{0,4},{4,0},{8,12},{12,8},{16,20},{20,16},{24,28},{28,24},{1,5},{5... | collective-permute-start | bytes 528392 | tf_op jit(solution)/shard_map/ppermute | solution.py:132
  41.8 1.6 %collective-permute-done.25.refs_26_ = bf16[344,256]{1,0:T(8,128)(2,1)S(1)} collective-permute-done((bf16[344,256]{1,0:T(8,128)(2,1)S(1)}, bf16[344,256]{1,0:T(8,128)(2,1)S(1)}, u32[]{:S(2)}, u32[]{:S(2)}) %collective-permute-start.25) | collective-permute-done | bytes 176160 | tf_op jit(solution)/shard_map/ppermute | solution.py:132
  43.3 0.5 collective-permute-start.30
  43.9 3.0 %collective-permute-done.13.refs_14_ = bf16[344,256]{1,0:T(8,128)(2,1)S(1)} collective-permute-done((bf16[344,256]{1,0:T(8,128)(2,1)S(1)}, bf16[344,256]{1,0:T(8,128)(2,1)S(1)}, u32[]{:S(2)}, u32[]{:S(2)}) %collective-permute-start.13) | collective-permute-done | bytes 176160 | tf_op jit(solution)/shard_map/ppermute | solution.py:132
  46.9 0.5 collective-permute-start.26
  47.5 1.0 %copy-done.2 = bf16[512,512]{1,0:T(8,128)(2,1)S(1)} copy-done((bf16[512,512]{1,0:T(8,128)(2,1)S(1)}, bf16[512,512]{1,0:T(8,128)(2,1)}, u32[]{:S(2)}) %copy-start.2) | copy-done | bytes 524312
  48.6 0.9 %copy-done.3 = f32[256,128]{1,0:T(8,128)S(1)} copy-done((f32[256,128]{1,0:T(8,128)S(1)}, f32[256,128]{1,0:T(8,128)}, u32[]{:S(2)}) %copy-start.3) | copy-done | bytes 131096
  49.5 0.7 copy-done.4
  50.2 1.3 %stage.1 = (bf16[1536,384]{1,0:T(8,128)(2,1)S(1)}, bf16[512,512]{1,0:T(8,128)(2,1)S(1)}, f32[1536]{0:T(1024)S(1)}, f32[256,128]{1,0:T(8,128)S(1)}) custom-call(bf16[1536,3072]{1,0:T(8,128)(2,1)} %w_query_hbm.1, bf16[512,512]{1,0:T(8,128)(2,1)S(1)} %copy-done.2, f32[1536]{0:T(1024)S(1)} %copy-done.4, f32[256,128]{1,0:T(8,128)S(1)} %copy-done.3), custom_call_target="tpu_custom_call" | custom-call | tf_op jit(solution)/shard_map/stage/pallas_call | solution.py:253
  51.6 5.8 %attend.1.refs_0_ = bf16[256,256]{1,0:T(8,128)(2,1)S(1)} custom-call(bf16[344,256]{1,0:T(8,128)(2,1)S(1)} %copy-done.1, bf16[344,256]{1,0:T(8,128)(2,1)S(1)} %collective-permute-done.refs_1_, bf16[344,256]{1,0:T(8,128)(2,1)S(1)} %collective-permute-done.1.refs_2_, bf16[344,256]{1,0:T(8,128)(2,1)S(1)} %collective-permute-done.2.refs_3_, ...), custom_call_target="tpu_custom_call" | custom-call | tf_op jit(solution)/shard_map/attend/pallas_call | solution.py:417
  57.4 3.7 %collective-permute-start.34 = (bf16[256,256]{1,0:T(8,128)(2,1)S(1)}, bf16[256,256]{1,0:T(8,128)(2,1)S(1)}, u32[]{:S(2)}, u32[]{:S(2)}) collective-permute-start(bf16[256,256]{1,0:T(8,128)(2,1)S(1)} %attend.1.refs_0_), channel_id=1, source_target_pairs={{0,16},{4,20},{8,24},{12,28},{16,0},{20,4},{24,8},{28,12},{1,17},{... | collective-permute-start | bytes 393224 | tf_op jit(solution)/shard_map/ppermute | solution.py:132
  61.0 1.7 %collective-permute-start.31 = (bf16[256,256]{1,0:T(8,128)(2,1)S(1)}, bf16[256,256]{1,0:T(8,128)(2,1)S(1)}, u32[]{:S(2)}, u32[]{:S(2)}) collective-permute-start(bf16[256,256]{1,0:T(8,128)(2,1)S(1)} %attend.1.refs_0_), channel_id=1, source_target_pairs={{0,4},{4,0},{8,12},{12,8},{16,20},{20,16},{24,28},{28,24},{1,5},{5... | collective-permute-start | bytes 393224 | tf_op jit(solution)/shard_map/ppermute | solution.py:132
  62.8 4.6 %collective-permute-done.34.refs_4_ = bf16[256,256]{1,0:T(8,128)(2,1)S(1)} collective-permute-done((bf16[256,256]{1,0:T(8,128)(2,1)S(1)}, bf16[256,256]{1,0:T(8,128)(2,1)S(1)}, u32[]{:S(2)}, u32[]{:S(2)}) %collective-permute-start.34) | collective-permute-done | bytes 131104 | tf_op jit(solution)/shard_map/ppermute | solution.py:132
  67.4 0.9 collective-permute-start.37
  68.3 2.3 %collective-permute-start.36 = (bf16[256,256]{1,0:T(8,128)(2,1)S(1)}, bf16[256,256]{1,0:T(8,128)(2,1)S(1)}, u32[]{:S(2)}, u32[]{:S(2)}) collective-permute-start(bf16[256,256]{1,0:T(8,128)(2,1)S(1)} %collective-permute-done.34.refs_4_), channel_id=1, source_target_pairs={{0,8},{4,12},{8,0},{12,4},{16,24},{20,28},{24,16},{28,20},{1,9},{5... | collective-permute-start | bytes 393224 | tf_op jit(solution)/shard_map/ppermute | solution.py:132
  70.9 1.7 %collective-permute-start.33 = (bf16[256,256]{1,0:T(8,128)(2,1)S(1)}, bf16[256,256]{1,0:T(8,128)(2,1)S(1)}, u32[]{:S(2)}, u32[]{:S(2)}) collective-permute-start(bf16[256,256]{1,0:T(8,128)(2,1)S(1)} %collective-permute-done.32.refs_2_), channel_id=1, source_target_pairs={{0,4},{4,0},{8,12},{12,8},{16,20},{20,16},{24,28},{28,24},{1,5},{5... | collective-permute-start | bytes 393224 | tf_op jit(solution)/shard_map/ppermute | solution.py:132
  72.6 2.1 %collective-permute-done.37.refs_7_ = bf16[256,256]{1,0:T(8,128)(2,1)S(1)} collective-permute-done((bf16[256,256]{1,0:T(8,128)(2,1)S(1)}, bf16[256,256]{1,0:T(8,128)(2,1)S(1)}, u32[]{:S(2)}, u32[]{:S(2)}) %collective-permute-start.37) | collective-permute-done | bytes 131104 | tf_op jit(solution)/shard_map/ppermute | solution.py:132
  74.7 2.1 %collective-permute-done.36.refs_6_ = bf16[256,256]{1,0:T(8,128)(2,1)S(1)} collective-permute-done((bf16[256,256]{1,0:T(8,128)(2,1)S(1)}, bf16[256,256]{1,0:T(8,128)(2,1)S(1)}, u32[]{:S(2)}, u32[]{:S(2)}) %collective-permute-start.36) | collective-permute-done | bytes 131104 | tf_op jit(solution)/shard_map/ppermute | solution.py:132
  76.7 0.4 collective-permute-done.35.refs_5_
  77.2 2.2 %collective-permute-done.33.refs_3_ = bf16[256,256]{1,0:T(8,128)(2,1)S(1)} collective-permute-done((bf16[256,256]{1,0:T(8,128)(2,1)S(1)}, bf16[256,256]{1,0:T(8,128)(2,1)S(1)}, u32[]{:S(2)}, u32[]{:S(2)}) %collective-permute-start.33) | collective-permute-done | bytes 131104 | tf_op jit(solution)/shard_map/ppermute | solution.py:132
  79.4 1.3 %project_out.1 = (f32[64,896]{1,0:T(8,128)S(1)}, bf16[64,896]{1,0:T(8,128)(2,1)S(1)}, bf16[64,896]{1,0:T(8,128)(2,1)S(1)}, bf16[64,896]{1,0:T(8,128)(2,1)S(1)}) custom-call(bf16[256,256]{1,0:T(8,128)(2,1)S(1)} %attend.1.refs_0_, bf16[256,256]{1,0:T(8,128)(2,1)S(1)} %collective-permute-done.31.refs_1_, bf16[256,256]{1,0:T(8,128)(2,1)S(1)} %collective-permute-done.32.refs_2_, ...), custom_call_target="tpu_custom_call" | custom-call | tf_op jit(solution)/shard_map/project_out/pallas_call | solution.py:468
  80.8 2.1 %collective-permute-start.39 = (bf16[64,896]{1,0:T(8,128)(2,1)S(1)}, bf16[64,896]{1,0:T(8,128)(2,1)S(1)}, u32[]{:S(2)}, u32[]{:S(2)}) collective-permute-start(bf16[64,896]{1,0:T(8,128)(2,1)S(1)} %get-tuple-element.19), channel_id=1, source_target_pairs={{0,2},{1,3},{2,0},{3,1},{4,6},{5,7},{6,4},{7,5},{8,10},{9,11},{10,... | collective-permute-start | bytes 344072 | tf_op jit(solution)/shard_map/ppermute | solution.py:132
  82.9 4.0 %collective-permute-done.39 = bf16[64,896]{1,0:T(8,128)(2,1)S(1)} collective-permute-done((bf16[64,896]{1,0:T(8,128)(2,1)S(1)}, bf16[64,896]{1,0:T(8,128)(2,1)S(1)}, u32[]{:S(2)}, u32[]{:S(2)}) %collective-permute-start.39) | collective-permute-done | bytes 114720 | tf_op jit(solution)/shard_map/ppermute | solution.py:132
  86.9 1.9 %collective-permute-done.40 = bf16[64,896]{1,0:T(8,128)(2,1)S(1)} collective-permute-done((bf16[64,896]{1,0:T(8,128)(2,1)S(1)}, bf16[64,896]{1,0:T(8,128)(2,1)S(1)}, u32[]{:S(2)}, u32[]{:S(2)}) %collective-permute-start.40) | collective-permute-done | bytes 114720 | tf_op jit(solution)/shard_map/ppermute | solution.py:132
  88.8 0.7 add_convert_fusion
  (49 shorter events, 0.9 us)
Async XLA Ops:
  1.9 49.6 %copy-start.1 = (bf16[344,256]{1,0:T(8,128)(2,1)S(1)}, bf16[344,256]{1,0:T(8,128)(2,1)}, u32[]{:S(2)}) copy-start(bf16[344,256]{1,0:T(8,128)(2,1)} %pack.1.refs_0_) | copy-start | bytes 528388
  1.9 12.7 %collective-permute-start.15 = (bf16[344,256]{1,0:T(8,128)(2,1)}, bf16[344,256]{1,0:T(8,128)(2,1)S(1)}, u32[]{:S(2)}, u32[]{:S(2)}) collective-permute-start(bf16[344,256]{1,0:T(8,128)(2,1)} %pack.1.refs_0_), channel_id=1, source_target_pairs={{0,16},{4,20},{8,24},{12,28},{16,0},{20,4},{24,8},{28,12},{1,17},{... | collective-permute-start | bytes 528392 | tf_op jit(solution)/shard_map/ppermute | solution.py:132
  6.0 9.3 %collective-permute-start.7 = (bf16[344,256]{1,0:T(8,128)(2,1)}, bf16[344,256]{1,0:T(8,128)(2,1)S(1)}, u32[]{:S(2)}, u32[]{:S(2)}) collective-permute-start(bf16[344,256]{1,0:T(8,128)(2,1)} %pack.1.refs_0_), channel_id=1, source_target_pairs={{0,8},{4,12},{8,0},{12,4},{16,24},{20,28},{24,16},{28,20},{1,9},{5... | collective-permute-start | bytes 528392 | tf_op jit(solution)/shard_map/ppermute | solution.py:132
  7.6 9.2 %collective-permute-start.3 = (bf16[344,256]{1,0:T(8,128)(2,1)}, bf16[344,256]{1,0:T(8,128)(2,1)S(1)}, u32[]{:S(2)}, u32[]{:S(2)}) collective-permute-start(bf16[344,256]{1,0:T(8,128)(2,1)} %pack.1.refs_0_), channel_id=1, source_target_pairs={{0,4},{4,0},{8,12},{12,8},{16,20},{20,16},{24,28},{28,24},{1,5},{5... | collective-permute-start | bytes 528392 | tf_op jit(solution)/shard_map/ppermute | solution.py:132
  9.1 9.2 %collective-permute-start.1 = (bf16[344,256]{1,0:T(8,128)(2,1)}, bf16[344,256]{1,0:T(8,128)(2,1)S(1)}, u32[]{:S(2)}, u32[]{:S(2)}) collective-permute-start(bf16[344,256]{1,0:T(8,128)(2,1)} %pack.1.refs_0_), channel_id=1, source_target_pairs={{0,2},{1,3},{2,0},{3,1},{4,6},{5,7},{6,4},{7,5},{8,10},{9,11},{10,... | collective-permute-start | bytes 528392 | tf_op jit(solution)/shard_map/ppermute | solution.py:132
  10.6 7.7 %collective-permute-start = (bf16[344,256]{1,0:T(8,128)(2,1)}, bf16[344,256]{1,0:T(8,128)(2,1)S(1)}, u32[]{:S(2)}, u32[]{:S(2)}) collective-permute-start(bf16[344,256]{1,0:T(8,128)(2,1)} %pack.1.refs_0_), channel_id=1, source_target_pairs={{0,1},{1,0},{2,3},{3,2},{4,5},{5,4},{6,7},{7,6},{8,9},{9,8},{10,11... | collective-permute-start | bytes 528392 | tf_op jit(solution)/shard_map/ppermute | solution.py:132
  14.6 5.5 %collective-permute-start.23 = (bf16[344,256]{1,0:T(8,128)(2,1)S(1)}, bf16[344,256]{1,0:T(8,128)(2,1)S(1)}, u32[]{:S(2)}, u32[]{:S(2)}) collective-permute-start(bf16[344,256]{1,0:T(8,128)(2,1)S(1)} %collective-permute-done.15.refs_16_), channel_id=1, source_target_pairs={{0,8},{4,12},{8,0},{12,4},{16,24},{20,28},{24,16},{28,20},{1,9},{5... | collective-permute-start | bytes 528392 | tf_op jit(solution)/shard_map/ppermute | solution.py:132
  15.3 6.3 %collective-permute-start.19 = (bf16[344,256]{1,0:T(8,128)(2,1)S(1)}, bf16[344,256]{1,0:T(8,128)(2,1)S(1)}, u32[]{:S(2)}, u32[]{:S(2)}) collective-permute-start(bf16[344,256]{1,0:T(8,128)(2,1)S(1)} %collective-permute-done.15.refs_16_), channel_id=1, source_target_pairs={{0,4},{4,0},{8,12},{12,8},{16,20},{20,16},{24,28},{28,24},{1,5},{5... | collective-permute-start | bytes 528392 | tf_op jit(solution)/shard_map/ppermute | solution.py:132
  16.8 6.8 %collective-permute-start.17 = (bf16[344,256]{1,0:T(8,128)(2,1)S(1)}, bf16[344,256]{1,0:T(8,128)(2,1)S(1)}, u32[]{:S(2)}, u32[]{:S(2)}) collective-permute-start(bf16[344,256]{1,0:T(8,128)(2,1)S(1)} %collective-permute-done.15.refs_16_), channel_id=1, source_target_pairs={{0,2},{1,3},{2,0},{3,1},{4,6},{5,7},{6,4},{7,5},{8,10},{9,11},{10,... | collective-permute-start | bytes 528392 | tf_op jit(solution)/shard_map/ppermute | solution.py:132
  18.3 7.3 %collective-permute-start.16 = (bf16[344,256]{1,0:T(8,128)(2,1)S(1)}, bf16[344,256]{1,0:T(8,128)(2,1)S(1)}, u32[]{:S(2)}, u32[]{:S(2)}) collective-permute-start(bf16[344,256]{1,0:T(8,128)(2,1)S(1)} %collective-permute-done.15.refs_16_), channel_id=1, source_target_pairs={{0,1},{1,0},{2,3},{3,2},{4,5},{5,4},{6,7},{7,6},{8,9},{9,8},{10,11... | collective-permute-start | bytes 528392 | tf_op jit(solution)/shard_map/ppermute | solution.py:132
  18.3 7.3 %collective-permute-start.11 = (bf16[344,256]{1,0:T(8,128)(2,1)S(1)}, bf16[344,256]{1,0:T(8,128)(2,1)S(1)}, u32[]{:S(2)}, u32[]{:S(2)}) collective-permute-start(bf16[344,256]{1,0:T(8,128)(2,1)S(1)} %collective-permute-done.7.refs_8_), channel_id=1, source_target_pairs={{0,4},{4,0},{8,12},{12,8},{16,20},{20,16},{24,28},{28,24},{1,5},{5... | collective-permute-start | bytes 528392 | tf_op jit(solution)/shard_map/ppermute | solution.py:132
  20.1 7.3 %collective-permute-start.9 = (bf16[344,256]{1,0:T(8,128)(2,1)S(1)}, bf16[344,256]{1,0:T(8,128)(2,1)S(1)}, u32[]{:S(2)}, u32[]{:S(2)}) collective-permute-start(bf16[344,256]{1,0:T(8,128)(2,1)S(1)} %collective-permute-done.7.refs_8_), channel_id=1, source_target_pairs={{0,2},{1,3},{2,0},{3,1},{4,6},{5,7},{6,4},{7,5},{8,10},{9,11},{10,... | collective-permute-start | bytes 528392 | tf_op jit(solution)/shard_map/ppermute | solution.py:132
  21.6 6.4 %collective-permute-start.8 = (bf16[344,256]{1,0:T(8,128)(2,1)S(1)}, bf16[344,256]{1,0:T(8,128)(2,1)S(1)}, u32[]{:S(2)}, u32[]{:S(2)}) collective-permute-start(bf16[344,256]{1,0:T(8,128)(2,1)S(1)} %collective-permute-done.7.refs_8_), channel_id=1, source_target_pairs={{0,1},{1,0},{2,3},{3,2},{4,5},{5,4},{6,7},{7,6},{8,9},{9,8},{10,11... | collective-permute-start | bytes 528392 | tf_op jit(solution)/shard_map/ppermute | solution.py:132
  23.6 10.5 %collective-permute-start.5 = (bf16[344,256]{1,0:T(8,128)(2,1)S(1)}, bf16[344,256]{1,0:T(8,128)(2,1)S(1)}, u32[]{:S(2)}, u32[]{:S(2)}) collective-permute-start(bf16[344,256]{1,0:T(8,128)(2,1)S(1)} %collective-permute-done.3.refs_4_), channel_id=1, source_target_pairs={{0,2},{1,3},{2,0},{3,1},{4,6},{5,7},{6,4},{7,5},{8,10},{9,11},{10,... | collective-permute-start | bytes 528392 | tf_op jit(solution)/shard_map/ppermute | solution.py:132
  25.7 9.4 %collective-permute-start.4 = (bf16[344,256]{1,0:T(8,128)(2,1)S(1)}, bf16[344,256]{1,0:T(8,128)(2,1)S(1)}, u32[]{:S(2)}, u32[]{:S(2)}) collective-permute-start(bf16[344,256]{1,0:T(8,128)(2,1)S(1)} %collective-permute-done.3.refs_4_), channel_id=1, source_target_pairs={{0,1},{1,0},{2,3},{3,2},{4,5},{5,4},{6,7},{7,6},{8,9},{9,8},{10,11... | collective-permute-start | bytes 528392 | tf_op jit(solution)/shard_map/ppermute | solution.py:132
  25.7 10.0 %collective-permute-start.2 = (bf16[344,256]{1,0:T(8,128)(2,1)S(1)}, bf16[344,256]{1,0:T(8,128)(2,1)S(1)}, u32[]{:S(2)}, u32[]{:S(2)}) collective-permute-start(bf16[344,256]{1,0:T(8,128)(2,1)S(1)} %collective-permute-done.1.refs_2_), channel_id=1, source_target_pairs={{0,1},{1,0},{2,3},{3,2},{4,5},{5,4},{6,7},{7,6},{8,9},{9,8},{10,11... | collective-permute-start | bytes 528392 | tf_op jit(solution)/shard_map/ppermute | solution.py:132
  27.4 8.3 %collective-permute-start.29 = (bf16[344,256]{1,0:T(8,128)(2,1)S(1)}, bf16[344,256]{1,0:T(8,128)(2,1)S(1)}, u32[]{:S(2)}, u32[]{:S(2)}) collective-permute-start(bf16[344,256]{1,0:T(8,128)(2,1)S(1)} %collective-permute-done.23.refs_24_), channel_id=1, source_target_pairs={{0,6},{1,7},{2,4},{3,5},{4,2},{5,3},{6,0},{7,1},{8,14},{9,15},{10,... | collective-permute-start | bytes 528392 | tf_op jit(solution)/shard_map/ppermute | solution.py:132
  28.0 9.8 %collective-permute-start.24 = (bf16[344,256]{1,0:T(8,128)(2,1)S(1)}, bf16[344,256]{1,0:T(8,128)(2,1)S(1)}, u32[]{:S(2)}, u32[]{:S(2)}) collective-permute-start(bf16[344,256]{1,0:T(8,128)(2,1)S(1)} %collective-permute-done.23.refs_24_), channel_id=1, source_target_pairs={{0,1},{1,0},{2,3},{3,2},{4,5},{5,4},{6,7},{7,6},{8,9},{9,8},{10,11... | collective-permute-start | bytes 528392 | tf_op jit(solution)/shard_map/ppermute | solution.py:132
  34.1 5.9 %collective-permute-start.27 = (bf16[344,256]{1,0:T(8,128)(2,1)S(1)}, bf16[344,256]{1,0:T(8,128)(2,1)S(1)}, u32[]{:S(2)}, u32[]{:S(2)}) collective-permute-start(bf16[344,256]{1,0:T(8,128)(2,1)S(1)} %collective-permute-done.19.refs_20_), channel_id=1, source_target_pairs={{0,8},{4,12},{8,0},{12,4},{16,24},{20,28},{24,16},{28,20},{1,9},{5... | collective-permute-start | bytes 528392 | tf_op jit(solution)/shard_map/ppermute | solution.py:132
  35.1 5.5 %collective-permute-start.21 = (bf16[344,256]{1,0:T(8,128)(2,1)S(1)}, bf16[344,256]{1,0:T(8,128)(2,1)S(1)}, u32[]{:S(2)}, u32[]{:S(2)}) collective-permute-start(bf16[344,256]{1,0:T(8,128)(2,1)S(1)} %collective-permute-done.19.refs_20_), channel_id=1, source_target_pairs={{0,2},{1,3},{2,0},{3,1},{4,6},{5,7},{6,4},{7,5},{8,10},{9,11},{10,... | collective-permute-start | bytes 528392 | tf_op jit(solution)/shard_map/ppermute | solution.py:132
  35.7 6.1 %collective-permute-start.20 = (bf16[344,256]{1,0:T(8,128)(2,1)S(1)}, bf16[344,256]{1,0:T(8,128)(2,1)S(1)}, u32[]{:S(2)}, u32[]{:S(2)}) collective-permute-start(bf16[344,256]{1,0:T(8,128)(2,1)S(1)} %collective-permute-done.19.refs_20_), channel_id=1, source_target_pairs={{0,1},{1,0},{2,3},{3,2},{4,5},{5,4},{6,7},{7,6},{8,9},{9,8},{10,11... | collective-permute-start | bytes 528392 | tf_op jit(solution)/shard_map/ppermute | solution.py:132
  35.7 7.6 %collective-permute-start.25 = (bf16[344,256]{1,0:T(8,128)(2,1)S(1)}, bf16[344,256]{1,0:T(8,128)(2,1)S(1)}, u32[]{:S(2)}, u32[]{:S(2)}) collective-permute-start(bf16[344,256]{1,0:T(8,128)(2,1)S(1)} %collective-permute-done.17.refs_18_), channel_id=1, source_target_pairs={{0,8},{4,12},{8,0},{12,4},{16,24},{20,28},{24,16},{28,20},{1,9},{5... | collective-permute-start | bytes 528392 | tf_op jit(solution)/shard_map/ppermute | solution.py:132
  37.8 5.6 %collective-permute-start.18 = (bf16[344,256]{1,0:T(8,128)(2,1)S(1)}, bf16[344,256]{1,0:T(8,128)(2,1)S(1)}, u32[]{:S(2)}, u32[]{:S(2)}) collective-permute-start(bf16[344,256]{1,0:T(8,128)(2,1)S(1)} %collective-permute-done.17.refs_18_), channel_id=1, source_target_pairs={{0,1},{1,0},{2,3},{3,2},{4,5},{5,4},{6,7},{7,6},{8,9},{9,8},{10,11... | collective-permute-start | bytes 528392 | tf_op jit(solution)/shard_map/ppermute | solution.py:132
  40.0 3.8 %collective-permute-start.12 = (bf16[344,256]{1,0:T(8,128)(2,1)S(1)}, bf16[344,256]{1,0:T(8,128)(2,1)S(1)}, u32[]{:S(2)}, u32[]{:S(2)}) collective-permute-start(bf16[344,256]{1,0:T(8,128)(2,1)S(1)} %collective-permute-done.11.refs_12_), channel_id=1, source_target_pairs={{0,1},{1,0},{2,3},{3,2},{4,5},{5,4},{6,7},{7,6},{8,9},{9,8},{10,11... | collective-permute-start | bytes 528392 | tf_op jit(solution)/shard_map/ppermute | solution.py:132
  40.5 6.4 %collective-permute-start.13 = (bf16[344,256]{1,0:T(8,128)(2,1)S(1)}, bf16[344,256]{1,0:T(8,128)(2,1)S(1)}, u32[]{:S(2)}, u32[]{:S(2)}) collective-permute-start(bf16[344,256]{1,0:T(8,128)(2,1)S(1)} %collective-permute-done.9.refs_10_), channel_id=1, source_target_pairs={{0,4},{4,0},{8,12},{12,8},{16,20},{20,16},{24,28},{28,24},{1,5},{5... | collective-permute-start | bytes 528392 | tf_op jit(solution)/shard_map/ppermute | solution.py:132
  41.8 5.2 %collective-permute-start.10 = (bf16[344,256]{1,0:T(8,128)(2,1)S(1)}, bf16[344,256]{1,0:T(8,128)(2,1)S(1)}, u32[]{:S(2)}, u32[]{:S(2)}) collective-permute-start(bf16[344,256]{1,0:T(8,128)(2,1)S(1)} %collective-permute-done.9.refs_10_), channel_id=1, source_target_pairs={{0,1},{1,0},{2,3},{3,2},{4,5},{5,4},{6,7},{7,6},{8,9},{9,8},{10,11... | collective-permute-start | bytes 528392 | tf_op jit(solution)/shard_map/ppermute | solution.py:132
  43.3 4.1 %collective-permute-start.6 = (bf16[344,256]{1,0:T(8,128)(2,1)S(1)}, bf16[344,256]{1,0:T(8,128)(2,1)S(1)}, u32[]{:S(2)}, u32[]{:S(2)}) collective-permute-start(bf16[344,256]{1,0:T(8,128)(2,1)S(1)} %collective-permute-done.5.refs_6_), channel_id=1, source_target_pairs={{0,1},{1,0},{2,3},{3,2},{4,5},{5,4},{6,7},{7,6},{8,9},{9,8},{10,11... | collective-permute-start | bytes 528392 | tf_op jit(solution)/shard_map/ppermute | solution.py:132
  43.3 8.1 %collective-permute-start.30 = (bf16[344,256]{1,0:T(8,128)(2,1)S(1)}, bf16[344,256]{1,0:T(8,128)(2,1)S(1)}, u32[]{:S(2)}, u32[]{:S(2)}) collective-permute-start(bf16[344,256]{1,0:T(8,128)(2,1)S(1)} %collective-permute-done.29.refs_30_), channel_id=1, source_target_pairs={{0,1},{1,0},{2,3},{3,2},{4,5},{5,4},{6,7},{7,6},{8,9},{9,8},{10,11... | collective-permute-start | bytes 528392 | tf_op jit(solution)/shard_map/ppermute | solution.py:132
  43.9 7.6 %collective-permute-start.28 = (bf16[344,256]{1,0:T(8,128)(2,1)S(1)}, bf16[344,256]{1,0:T(8,128)(2,1)S(1)}, u32[]{:S(2)}, u32[]{:S(2)}) collective-permute-start(bf16[344,256]{1,0:T(8,128)(2,1)S(1)} %collective-permute-done.27.refs_28_), channel_id=1, source_target_pairs={{0,1},{1,0},{2,3},{3,2},{4,5},{5,4},{6,7},{7,6},{8,9},{9,8},{10,11... | collective-permute-start | bytes 528392 | tf_op jit(solution)/shard_map/ppermute | solution.py:132
  46.9 4.6 %collective-permute-start.22 = (bf16[344,256]{1,0:T(8,128)(2,1)S(1)}, bf16[344,256]{1,0:T(8,128)(2,1)S(1)}, u32[]{:S(2)}, u32[]{:S(2)}) collective-permute-start(bf16[344,256]{1,0:T(8,128)(2,1)S(1)} %collective-permute-done.21.refs_22_), channel_id=1, source_target_pairs={{0,1},{1,0},{2,3},{3,2},{4,5},{5,4},{6,7},{7,6},{8,9},{9,8},{10,11... | collective-permute-start | bytes 528392 | tf_op jit(solution)/shard_map/ppermute | solution.py:132
  46.9 4.6 %collective-permute-start.26 = (bf16[344,256]{1,0:T(8,128)(2,1)S(1)}, bf16[344,256]{1,0:T(8,128)(2,1)S(1)}, u32[]{:S(2)}, u32[]{:S(2)}) collective-permute-start(bf16[344,256]{1,0:T(8,128)(2,1)S(1)} %collective-permute-done.25.refs_26_), channel_id=1, source_target_pairs={{0,1},{1,0},{2,3},{3,2},{4,5},{5,4},{6,7},{7,6},{8,9},{9,8},{10,11... | collective-permute-start | bytes 528392 | tf_op jit(solution)/shard_map/ppermute | solution.py:132
  47.4 4.1 %collective-permute-start.14 = (bf16[344,256]{1,0:T(8,128)(2,1)S(1)}, bf16[344,256]{1,0:T(8,128)(2,1)S(1)}, u32[]{:S(2)}, u32[]{:S(2)}) collective-permute-start(bf16[344,256]{1,0:T(8,128)(2,1)S(1)} %collective-permute-done.13.refs_14_), channel_id=1, source_target_pairs={{0,1},{1,0},{2,3},{3,2},{4,5},{5,4},{6,7},{7,6},{8,9},{9,8},{10,11... | collective-permute-start | bytes 528392 | tf_op jit(solution)/shard_map/ppermute | solution.py:132
  47.5 1.0 %copy-start.2 = (bf16[512,512]{1,0:T(8,128)(2,1)S(1)}, bf16[512,512]{1,0:T(8,128)(2,1)}, u32[]{:S(2)}) copy-start(bf16[512,512]{1,0:T(8,128)(2,1)} %w_kv_hbm.1) | copy-start | bytes 1572868
  48.6 0.9 %copy-start.3 = (f32[256,128]{1,0:T(8,128)S(1)}, f32[256,128]{1,0:T(8,128)}, u32[]{:S(2)}) copy-start(f32[256,128]{1,0:T(8,128)} %constant.2.clone.turn_hbm) | copy-start | bytes 393220
  49.5 0.7 copy-start.4
  51.5 27.8 %copy-start = (bf16[2048,896]{1,0:T(8,128)(2,1)S(1)}, bf16[2048,896]{1,0:T(8,128)(2,1)}, u32[]{:S(2)}) copy-start(bf16[2048,896]{1,0:T(8,128)(2,1)} %refs_8_.1) | copy-start | bytes 11010052
  57.4 10.0 %collective-permute-start.34 = (bf16[256,256]{1,0:T(8,128)(2,1)S(1)}, bf16[256,256]{1,0:T(8,128)(2,1)S(1)}, u32[]{:S(2)}, u32[]{:S(2)}) collective-permute-start(bf16[256,256]{1,0:T(8,128)(2,1)S(1)} %attend.1.refs_0_), channel_id=1, source_target_pairs={{0,16},{4,20},{8,24},{12,28},{16,0},{20,4},{24,8},{28,12},{1,17},{... | collective-permute-start | bytes 393224 | tf_op jit(solution)/shard_map/ppermute | solution.py:132
  61.0 9.8 %collective-permute-start.32 = (bf16[256,256]{1,0:T(8,128)(2,1)S(1)}, bf16[256,256]{1,0:T(8,128)(2,1)S(1)}, u32[]{:S(2)}, u32[]{:S(2)}) collective-permute-start(bf16[256,256]{1,0:T(8,128)(2,1)S(1)} %attend.1.refs_0_), channel_id=1, source_target_pairs={{0,8},{4,12},{8,0},{12,4},{16,24},{20,28},{24,16},{28,20},{1,9},{5... | collective-permute-start | bytes 393224 | tf_op jit(solution)/shard_map/ppermute | solution.py:132
  61.0 11.5 %collective-permute-start.31 = (bf16[256,256]{1,0:T(8,128)(2,1)S(1)}, bf16[256,256]{1,0:T(8,128)(2,1)S(1)}, u32[]{:S(2)}, u32[]{:S(2)}) collective-permute-start(bf16[256,256]{1,0:T(8,128)(2,1)S(1)} %attend.1.refs_0_), channel_id=1, source_target_pairs={{0,4},{4,0},{8,12},{12,8},{16,20},{20,16},{24,28},{28,24},{1,5},{5... | collective-permute-start | bytes 393224 | tf_op jit(solution)/shard_map/ppermute | solution.py:132
  67.4 7.3 %collective-permute-start.37 = (bf16[256,256]{1,0:T(8,128)(2,1)S(1)}, bf16[256,256]{1,0:T(8,128)(2,1)S(1)}, u32[]{:S(2)}, u32[]{:S(2)}) collective-permute-start(bf16[256,256]{1,0:T(8,128)(2,1)S(1)} %collective-permute-done.34.refs_4_), channel_id=1, source_target_pairs={{0,12},{4,8},{8,4},{12,0},{16,28},{20,24},{24,20},{28,16},{1,13},{... | collective-permute-start | bytes 393224 | tf_op jit(solution)/shard_map/ppermute | solution.py:132
  68.3 8.5 %collective-permute-start.36 = (bf16[256,256]{1,0:T(8,128)(2,1)S(1)}, bf16[256,256]{1,0:T(8,128)(2,1)S(1)}, u32[]{:S(2)}, u32[]{:S(2)}) collective-permute-start(bf16[256,256]{1,0:T(8,128)(2,1)S(1)} %collective-permute-done.34.refs_4_), channel_id=1, source_target_pairs={{0,8},{4,12},{8,0},{12,4},{16,24},{20,28},{24,16},{28,20},{1,9},{5... | collective-permute-start | bytes 393224 | tf_op jit(solution)/shard_map/ppermute | solution.py:132
  70.5 6.7 %collective-permute-start.35 = (bf16[256,256]{1,0:T(8,128)(2,1)S(1)}, bf16[256,256]{1,0:T(8,128)(2,1)S(1)}, u32[]{:S(2)}, u32[]{:S(2)}) collective-permute-start(bf16[256,256]{1,0:T(8,128)(2,1)S(1)} %collective-permute-done.34.refs_4_), channel_id=1, source_target_pairs={{0,4},{4,0},{8,12},{12,8},{16,20},{20,16},{24,28},{28,24},{1,5},{5... | collective-permute-start | bytes 393224 | tf_op jit(solution)/shard_map/ppermute | solution.py:132
  70.9 8.5 %collective-permute-start.33 = (bf16[256,256]{1,0:T(8,128)(2,1)S(1)}, bf16[256,256]{1,0:T(8,128)(2,1)S(1)}, u32[]{:S(2)}, u32[]{:S(2)}) collective-permute-start(bf16[256,256]{1,0:T(8,128)(2,1)S(1)} %collective-permute-done.32.refs_2_), channel_id=1, source_target_pairs={{0,4},{4,0},{8,12},{12,8},{16,20},{20,16},{24,28},{28,24},{1,5},{5... | collective-permute-start | bytes 393224 | tf_op jit(solution)/shard_map/ppermute | solution.py:132
  80.7 2.2 %collective-permute-start.38 = (bf16[64,896]{1,0:T(8,128)(2,1)S(1)}, bf16[64,896]{1,0:T(8,128)(2,1)S(1)}, u32[]{:S(2)}, u32[]{:S(2)}) collective-permute-start(bf16[64,896]{1,0:T(8,128)(2,1)S(1)} %get-tuple-element.18), channel_id=1, source_target_pairs={{0,1},{1,0},{2,3},{3,2},{4,5},{5,4},{6,7},{7,6},{8,9},{9,8},{10,11... | collective-permute-start | bytes 344072 | tf_op jit(solution)/shard_map/ppermute | solution.py:132
  80.8 6.1 %collective-permute-start.39 = (bf16[64,896]{1,0:T(8,128)(2,1)S(1)}, bf16[64,896]{1,0:T(8,128)(2,1)S(1)}, u32[]{:S(2)}, u32[]{:S(2)}) collective-permute-start(bf16[64,896]{1,0:T(8,128)(2,1)S(1)} %get-tuple-element.19), channel_id=1, source_target_pairs={{0,2},{1,3},{2,0},{3,1},{4,6},{5,7},{6,4},{7,5},{8,10},{9,11},{10,... | collective-permute-start | bytes 344072 | tf_op jit(solution)/shard_map/ppermute | solution.py:132
  82.9 5.9 %collective-permute-start.40 = (bf16[64,896]{1,0:T(8,128)(2,1)S(1)}, bf16[64,896]{1,0:T(8,128)(2,1)S(1)}, u32[]{:S(2)}, u32[]{:S(2)}) collective-permute-start(bf16[64,896]{1,0:T(8,128)(2,1)S(1)} %get-tuple-element.20), channel_id=1, source_target_pairs={{0,3},{1,2},{2,1},{3,0},{4,7},{5,6},{6,5},{7,4},{8,11},{9,10},{10,... | collective-permute-start | bytes 344072 | tf_op jit(solution)/shard_map/ppermute | solution.py:132
